TPU v7x, 32 devices: a whole 2x2x4 slice. The times are simulated.
32 devices in a mesh: chan: 8 (over z, x), blk: 4 (over y, core).
Axes of the slice: x: 2, y: 2, z: 4, core: 2. Of those that a mesh axis runs over, the one named last changes fastest.
Arguments:
- omega: float32 [8, 576, 576], P('chan', 'blk'), may hold values from -0.25 to 0.25
- hamiltonian: float32 [8, 576, 576], P('chan', 'blk'), may hold values from -6 to 6
- pair_occ: float32 [8, 576], P('chan'), may hold values from -1 to 1
- cross_occ: float32 [8, 576], P('chan'), may hold values from -1 to 1
- block_size: int32 [8], P('chan'), may hold values from 288 to 576
- jlabel: int32 [8], replicated, may hold values from 0 to 7
- family: int32 [8], replicated, may hold values from 0 to 3
- sixj: float32 [8, 8], replicated, may hold values from -4 to 4
- column_map: int32 [576], replicated, may hold values from 0 to 575, each once
Outputs:
- evolved: float32 [8, 576, 576], P('chan', 'blk')
Inputs may be any that keep to these rules, and one draw needn't show every extreme that they name: `column_map`: a permutation of 0 to 575.
All inputs are finite; a program needn't handle non-finite values.
Results may differ from a plain program's by a relative error of at most 0.0032.
Values may be sent and summed in bfloat16 or wider, within the bound.
No kernel may reach another device: no remote copies, remote signals or barrier semaphores. Data moves between devices by JAX's collectives and lax.ppermute only.
A program may use at most 64 MiB of HBM per device.

v0:
```python
import jax
import jax.numpy as jnp
from jax import lax
from jax.sharding import PartitionSpec as P

exact_mode = lax.Precision.HIGHEST


def mixing_matrix(jlabel, family, sixj):
    levels = sixj.shape[0]
    one_hot = (jlabel[:, None] == jnp.arange(levels, dtype=jnp.int32)[None, :]).astype(jnp.float32)
    picked = jnp.dot(one_hot, sixj, precision=exact_mode, preferred_element_type=jnp.float32)
    picked = jnp.dot(picked, one_hot.T, precision=exact_mode, preferred_element_type=jnp.float32)
    kindred = (family[:, None] == family[None, :]).astype(jnp.float32)
    return picked * kindred


def commutator(left_rows, left_full, right_rows, weights):
    scaled_left = (left_rows * weights[:, None, :]).astype(jnp.bfloat16)
    scaled_right = (right_rows * weights[:, None, :]).astype(jnp.bfloat16)
    initial = -jnp.einsum(
        "crk,ckq->crq", scaled_right, left_full, preferred_element_type=jnp.float32
    )
    return initial + jnp.einsum(
        "crk,ckq->crq",
        scaled_left,
        lax.all_gather(right_rows.astype(jnp.bfloat16), "blk", axis=1, tiled=True),
        preferred_element_type=jnp.float32,
    )


def through_mixing(stacked, apply_fn):
    chan_size = lax.axis_size("chan")
    members, channels_here, rows_here, block_width = stacked.shape
    shaped = stacked.reshape(
        members, channels_here, chan_size, rows_here * block_width // chan_size
    )
    returned = lax.all_to_all(
        apply_fn(lax.all_to_all(shaped, "chan", split_axis=2, concat_axis=1, tiled=True)),
        "chan",
        split_axis=1,
        concat_axis=2,
        tiled=True,
    )
    return returned.reshape(returned.shape[0], channels_here, rows_here, block_width)


def on_device(
    omega, hamiltonian, pair_occ, cross_occ, block_size, jlabel, family, sixj, column_map
):
    channels_here, rows_here, block_width = omega.shape
    mixing = mixing_matrix(jlabel, family, sixj)
    row_index = lax.axis_index("blk") * rows_here + jnp.arange(rows_here, dtype=jnp.int32)
    col_index = jnp.arange(block_width, dtype=jnp.int32)
    inside_block = (row_index[None, :, None] < block_size[:, None, None]) & (
        col_index[None, None, :] < block_size[:, None, None]
    )
    window_mask = inside_block.astype(jnp.float32)
    generator = omega * window_mask
    start_ham = hamiltonian * window_mask
    inverse_map = jnp.argsort(column_map)

    def forward_mix(received):
        return jnp.einsum(
            "kc,scil->skil",
            mixing,
            received,
            precision=exact_mode,
            preferred_element_type=jnp.float32,
        )

    def reverse_mix(received):
        return jnp.einsum(
            "ck,scil->skil",
            mixing,
            received,
            precision=exact_mode,
            preferred_element_type=jnp.float32,
        )

    crossed = through_mixing(
        jnp.stack([generator[:, :, column_map], start_ham[:, :, column_map]]), forward_mix
    )
    gen_cross = crossed[0]
    ham_cross = crossed[1]
    gen_full = lax.all_gather(generator.astype(jnp.bfloat16), "blk", axis=1, tiled=True)
    first_pp = commutator(generator, gen_full, start_ham, pair_occ)
    cross_full = lax.all_gather(gen_cross.astype(jnp.bfloat16), "blk", axis=1, tiled=True)
    first_cc = commutator(gen_cross, cross_full, ham_cross, cross_occ)

    def both_mix(received):
        restored = jnp.einsum(
            "ck,cil->kil",
            mixing,
            received[1],
            precision=exact_mode,
            preferred_element_type=jnp.float32,
        )
        combined = jnp.einsum(
            "kc,cil->kil",
            mixing,
            received[0] + restored,
            precision=exact_mode,
            preferred_element_type=jnp.float32,
        )
        return jnp.stack([restored, combined])

    outcome = through_mixing(jnp.stack([first_pp[:, :, column_map], first_cc]), both_mix)
    eta = first_pp + outcome[0][:, :, inverse_map]
    eta_cross = outcome[1]
    second_pp = commutator(generator, gen_full, eta, pair_occ)
    second_cc = commutator(gen_cross, cross_full, eta_cross, cross_occ)
    second_back = through_mixing(second_cc[None], reverse_mix)[0]
    second = second_pp + second_back[:, :, inverse_map]
    return (start_ham + eta + 0.5 * second) * window_mask


def solution(mesh):
    in_specs = (
        P("chan", "blk", None),
        P("chan", "blk", None),
        P("chan", None),
        P("chan", None),
        P("chan"),
        P(),
        P(),
        P(),
        P(),
    )
    out_specs = P("chan", "blk", None)
    return jax.shard_map(
        on_device, mesh=mesh, in_specs=in_specs, out_specs=out_specs, check_vma=False
    )
```

profile of v0, /device:TPU:0, one launch (start us, length us, event | category | flops | bytes accessed | tf_op | source)
XLA Modules:
  0.0 194.0 jit_solution(8203636028920695372)
XLA Ops:
  0.7 1.2 fusion.28
  2.7 2.2 %gather_fusion.1 = f32[576,144]{1,0:T(8,128)S(1)} fusion(f32[144,576]{0,1:T(8,128)S(1)} %copy.34, s32[1024]{0:T(1024)S(1)} %pad_clamp_fusion.1), kind=kCustom, calls=%fused_computation.1 | custom fusion | bytes 665856 | tf_op jit(solution)/shard_map/gather | solution.py:82
  5.4 2.2 %gather_fusion.2 = f32[576,144]{1,0:T(8,128)S(1)} fusion(f32[144,576]{0,1:T(8,128)S(1)} %copy.36, s32[1024]{0:T(1024)S(1)} %pad_clamp_fusion.1), kind=kCustom, calls=%fused_computation.2 | custom fusion | bytes 665856 | tf_op jit(solution)/shard_map/gather | solution.py:82
  8.1 1.2 copy.38
  9.2 7.4 %all-to-all-start = ((f32[2,1,8,10368]{3,0,1,2:T(2,128)}), f32[2,1,8,10368]{3,0,1,2:T(2,128)S(1)}, u32[]{:S(2)}, u32[]{:S(2)}) async-start(f32[2,1,8,10368]{3,0,1,2:T(2,128)} %copy.38), calls=%async_computation | async-start | bytes 1327104 | tf_op jit(solution)/shard_map/all_to_all | solution.py:39
  17.4 0.6 copy-done.16
  18.9 15.2 %all-to-all-done = f32[2,1,8,10368]{3,0,1,2:T(2,128)S(1)} async-done(((f32[2,1,8,10368]{3,0,1,2:T(2,128)}), f32[2,1,8,10368]{3,0,1,2:T(2,128)S(1)}, u32[]{:S(2)}, u32[]{:S(2)}) %all-to-all-start) | async-done | bytes 663584 | tf_op jit(solution)/shard_map/all_to_all | solution.py:39
  34.1 0.7 convolution_bitcast_fusion
  34.8 1.2 copy.40
  36.0 3.8 %all-to-all-start.1 = ((f32[2,8,1,10368]{3,0,2,1:T(2,128)}), f32[2,8,1,10368]{3,0,2,1:T(2,128)S(1)}, u32[]{:S(2)}, u32[]{:S(2)}) async-start(f32[2,8,1,10368]{3,0,2,1:T(2,128)} %copy.40), calls=%async_computation.1 | async-start | bytes 1327104 | tf_op jit(solution)/shard_map/all_to_all | solution.py:38
  39.9 8.4 %all_gather.19 = bf16[1,576,576]{2,1,0:T(8,128)(2,1)S(1)} all-gather(bf16[1,144,576]{2,1,0:T(8,128)(2,1)S(1)} %get-tuple-element.20), channel_id=1, replica_groups=mesh['chan'=8,'blk'=4] {'blk'}, dimensions={1}, use_global_device_ids=true | all-gather | bytes 829440 | tf_op jit(solution)/shard_map/all_gather | solution.py:27
  48.3 8.4 %all_gather.18 = bf16[1,576,576]{2,1,0:T(8,128)(2,1)S(1)} all-gather(bf16[1,144,576]{2,1,0:T(8,128)(2,1)S(1)} %get-tuple-element.19), channel_id=1, replica_groups=mesh['chan'=8,'blk'=4] {'blk'}, dimensions={1}, use_global_device_ids=true | all-gather | bytes 829440 | tf_op jit(solution)/shard_map/all_gather | solution.py:86
  57.8 2.8 %gather_fusion = f32[576,144]{1,0:T(8,128)} fusion(f32[144,576]{0,1:T(8,128)S(1)} %copy.32, s32[1024]{0:T(1024)S(1)} %pad_clamp_fusion.1), kind=kCustom, calls=%fused_computation | custom fusion | bytes 665856 | tf_op jit(solution)/shard_map/gather | solution.py:108
  60.6 1.3 copy.33
  61.9 0.9 stack.27
  62.8 4.1 %convert_reduce_fusion.4 = (bf16[8,10368]{1,0:T(8,128)(2,1)S(1)}, bf16[8,10368]{1,0:T(8,128)(2,1)S(1)}, bf16[8,10368]{1,0:T(8,128)(2,1)S(1)}, bf16[8,10368]{1,0:T(8,128)(2,1)}) fusion(f32[2,8,1,10368]{3,0,2,1:T(2,128)S(1)} %all-to-all-done.1, f32[10368]{0:T(1024)S(1)} %mul.107), kind=kLoop, calls=%fused_computation.56 | loop fusion | flops 497664 | bytes 1368576 | tf_op jit(solution)/shard_map/convert_element_type | solution.py:88
  67.4 8.4 %all_gather.21 = bf16[1,576,576]{2,1,0:T(8,128)(2,1)S(1)} all-gather(bf16[1,144,576]{2,1,0:T(8,128)(2,1)S(1)} %convert_element_type.109), channel_id=1, replica_groups=mesh['chan'=8,'blk'=4] {'blk'}, dimensions={1}, use_global_device_ids=true | all-gather | bytes 829440 | tf_op jit(solution)/shard_map/all_gather | solution.py:27
  75.8 0.9 convert_element_type.105
  76.7 8.8 %all_gather.20 = bf16[1,576,576]{2,1,0:T(8,128)(2,1)S(1)} all-gather(bf16[1,144,576]{2,1,0:T(8,128)(2,1)} %convert_element_type.105), channel_id=1, replica_groups=mesh['chan'=8,'blk'=4] {'blk'}, dimensions={1}, use_global_device_ids=true | all-gather | bytes 829440 | tf_op jit(solution)/shard_map/all_gather | solution.py:88
  85.5 1.8 convert_element_type.103
  88.6 0.9 stack.31
  89.6 1.0 pad_maximum_fusion.1
  90.6 0.7 copy.41
  91.3 24.1 %all_to_all.24 = f32[2,1,8,10368]{3,1,0,2:T(1,128)S(1)} all-to-all(f32[2,1,8,10368]{3,1,0,2:T(1,128)S(1)} %copy.41), channel_id=1, replica_groups=mesh['chan'=8,'blk'=4] {'chan'}, dimensions={2} | all-to-all | bytes 1327104 | tf_op jit(solution)/shard_map/all_to_all | solution.py:39
  117.4 20.8 %all_to_all.25 = f32[2,8,1,10368]{3,0,2,1:T(2,128)S(1)} all-to-all(f32[2,8,1,10368]{3,0,2,1:T(2,128)S(1)} %copy.43), channel_id=1, replica_groups=mesh['chan'=8,'blk'=4] {'chan'}, dimensions={1} | all-to-all | bytes 1327104 | tf_op jit(solution)/shard_map/all_to_all | solution.py:38
  138.2 2.5 %convert_reduce_fusion.1 = (bf16[8,10368]{1,0:T(8,128)(2,1)}, bf16[8,10368]{1,0:T(8,128)(2,1)}) fusion(f32[2,8,1,10368]{3,0,2,1:T(2,128)S(1)} %all_to_all.25, f32[10368]{0:T(1024)S(1)} %mul.107), kind=kLoop, calls=%fused_computation.53 | loop fusion | flops 248832 | bytes 705024 | tf_op jit(solution)/shard_map/convert_element_type | solution.py:20
  140.6 1.8 convert_element_type.116
  142.5 7.7 %all_gather.23 = bf16[1,576,576]{2,1,0:T(8,128)(2,1)S(1)} all-gather(bf16[1,144,576]{2,1,0:T(8,128)(2,1)} %convert_element_type.116), channel_id=1, replica_groups=mesh['chan'=8,'blk'=4] {'blk'}, dimensions={1}, use_global_device_ids=true | all-gather | bytes 829440 | tf_op jit(solution)/shard_map/all_gather | solution.py:27
  150.2 1.1 fusion.9
  151.3 1.1 convert_element_type.114
  152.4 2.1 %fusion.6 = f32[144,576]{1,0:T(8,128)} fusion(f32[144,576]{1,0:T(8,128)} %fusion.9, bf16[144,576]{1,0:T(8,128)(2,1)S(1)} %convert_element_type.114, bf16[1,576,576]{2,1,0:T(8,128)(2,1)S(1)} %all_gather.20), kind=kOutput, calls=%fused_computation.18 | convolution fusion | flops 95717376 | bytes 1492992 | tf_op jit(solution)/shard_map/crk,ckq->crq/dot_general | solution.py:21
  154.5 2.1 %reshape_broadcast_in_dim.4 = f32[1,1,8,10368]{3,1,0,2:T(1,128)} reshape(f32[144,576]{1,0:T(8,128)} %fusion.6) | data formatting | bytes 663552 | tf_op jit(solution)/shard_map/reshape;broadcast_in_dim | solution.py:35
  156.6 4.1 %all-to-all-start.4 = ((f32[1,1,8,10368]{3,1,0,2:T(1,128)}), f32[1,1,8,10368]{3,1,0,2:T(1,128)}, u32[]{:S(2)}, u32[]{:S(2)}) async-start(f32[1,1,8,10368]{3,1,0,2:T(1,128)} %reshape_broadcast_in_dim.4), calls=%async_computation.4 | async-start | bytes 663552 | tf_op jit(solution)/shard_map/all_to_all | solution.py:39
  160.7 0.7 copy-done.13
  161.4 4.4 %sort.17 = (s32[576]{0:T(1024)}, s32[576]{0:T(1024)S(1)}) sort(s32[576]{0:T(1024)S(1)} %copy-done.13, s32[576]{0:T(1024)S(1)} %iota.20), dimensions={0}, to_apply=%region_0.0 | sort | flops 5760 | bytes 9216 | tf_op jit(solution)/shard_map/jit(argsort)/sort | solution.py:61
  165.7 0.8 slice_reduce_fusion
  167.0 2.2 %gather_fusion.3 = f32[576,144]{1,0:T(8,128)S(1)} fusion(f32[144,576]{0,1:T(8,128)S(1)} %copy.44, s32[1024]{0:T(1024)S(1)} %pad_clamp_fusion), kind=kCustom, calls=%fused_computation.3 | custom fusion | bytes 665856 | tf_op jit(solution)/shard_map/gather | solution.py:109
  169.4 2.4 %all-to-all-done.4 = f32[1,1,8,10368]{3,1,0,2:T(1,128)} async-done(((f32[1,1,8,10368]{3,1,0,2:T(1,128)}), f32[1,1,8,10368]{3,1,0,2:T(1,128)}, u32[]{:S(2)}, u32[]{:S(2)}) %all-to-all-start.4) | async-done | bytes 331808 | tf_op jit(solution)/shard_map/all_to_all | solution.py:39
  171.8 1.4 convolution_bitcast_fusion.1
  173.3 1.1 copy.47
  174.3 3.6 %all-to-all-start.5 = ((f32[1,8,1,10368]{3,2,0,1:T(1,128)}), f32[1,8,1,10368]{3,2,0,1:T(1,128)S(1)}, u32[]{:S(2)}, u32[]{:S(2)}) async-start(f32[1,8,1,10368]{3,2,0,1:T(1,128)} %copy.47), calls=%async_computation.5 | async-start | bytes 663552 | tf_op jit(solution)/shard_map/all_to_all | solution.py:38
  178.0 8.4 %all-gather = bf16[576,576]{1,0:T(8,128)(2,1)S(1)} all-gather(bf16[144,576]{1,0:T(8,128)(2,1)S(1)} %fusion.40), channel_id=2, replica_groups=mesh['chan'=8,'blk'=4] {'blk'}, dimensions={0}, use_global_device_ids=true | all-gather | bytes 829440 | tf_op jit(solution)/shard_map/all_gather | solution.py:27
  186.4 1.2 fusion.46
  187.5 1.0 all-to-all-done.5
  188.5 0.8 reduce.9
  189.8 2.2 %gather_fusion.4 = f32[576,144]{1,0:T(8,128)S(1)} fusion(f32[144,576]{0,1:T(8,128)S(1)} %copy.48, s32[1024]{0:T(1024)S(1)} %pad_clamp_fusion), kind=kCustom, calls=%fused_computation.4 | custom fusion | bytes 665856 | tf_op jit(solution)/shard_map/gather | solution.py:114
  192.1 0.8 copy-done.3
  192.9 1.1 fusion.8
  (74 shorter events, 9.5 us)
Async XLA Ops:
  0.0 17.4 %copy-start = (f32[8,8]{1,0:T(8,128)S(1)}, f32[8,8]{1,0:T(8,128)}, u32[]{:S(2)}) copy-start(f32[8,8]{1,0:T(8,128)} %param.16) | copy-start | bytes 772
  0.7 56.4 %copy-start.8 = (pred[576]{0:T(1024)(128)(4,1)}, pred[576]{0:T(1024)(128)(4,1)S(1)}, u32[]{:S(2)}) copy-start(pred[576]{0:T(1024)(128)(4,1)S(1)} %iota_compare_fusion.3) | copy-start | bytes 1732
  0.7 56.4 %copy-start.10 = (pred[144]{0:T(512)(128)(4,1)}, pred[144]{0:T(512)(128)(4,1)S(1)}, u32[]{:S(2)}) copy-start(pred[144]{0:T(512)(128)(4,1)S(1)} %add_compare_fusion) | copy-start | bytes 436
  1.9 0.7 copy-start.12
  9.2 7.4 %copy-start.14 = (f32[1,576]{1,0:T(1,128)S(1)}, f32[1,576]{1,0:T(1,128)}, u32[]{:S(2)}) copy-start(f32[1,576]{1,0:T(1,128)} %param.12) | copy-start | bytes 6916
  9.2 24.9 %all-to-all-start = ((f32[2,1,8,10368]{3,0,1,2:T(2,128)}), f32[2,1,8,10368]{3,0,1,2:T(2,128)S(1)}, u32[]{:S(2)}, u32[]{:S(2)}) async-start(f32[2,1,8,10368]{3,0,1,2:T(2,128)} %copy.38), calls=%async_computation | async-start | bytes 1327104 | tf_op jit(solution)/shard_map/all_to_all | solution.py:39
  16.7 0.7 copy-start.15
  17.4 0.7 copy-start.16
  18.0 0.7 copy-start.17
  18.9 15.9 %copy-start.6 = (f32[8,8]{1,0:T(8,128)}, f32[8,8]{1,0:T(8,128)S(1)}, u32[]{:S(2)}) copy-start(f32[8,8]{1,0:T(8,128)S(1)} %convolution_select_fusion) | copy-start | bytes 772
  36.0 3.8 %copy-start.1 = (f32[1,144,576]{2,1,0:T(8,128)S(1)}, f32[1,144,576]{2,1,0:T(8,128)}, u32[]{:S(2)}) copy-start(f32[1,144,576]{2,1,0:T(8,128)} %param.10) | copy-start | bytes 995332
  36.0 3.8 %copy-start.2 = (f32[1,144,576]{2,1,0:T(8,128)S(1)}, f32[1,144,576]{2,1,0:T(8,128)}, u32[]{:S(2)}) copy-start(f32[1,144,576]{2,1,0:T(8,128)} %param.9) | copy-start | bytes 995332
  36.0 26.8 %all-to-all-start.1 = ((f32[2,8,1,10368]{3,0,2,1:T(2,128)}), f32[2,8,1,10368]{3,0,2,1:T(2,128)S(1)}, u32[]{:S(2)}, u32[]{:S(2)}) async-start(f32[2,8,1,10368]{3,0,2,1:T(2,128)} %copy.40), calls=%async_computation.1 | async-start | bytes 1327104 | tf_op jit(solution)/shard_map/all_to_all | solution.py:38
  87.4 0.9 copy-start.5
  88.6 1.0 copy-start.4
  115.4 0.7 copy-start.7
  156.6 15.2 %all-to-all-start.4 = ((f32[1,1,8,10368]{3,1,0,2:T(1,128)}), f32[1,1,8,10368]{3,1,0,2:T(1,128)}, u32[]{:S(2)}, u32[]{:S(2)}) async-start(f32[1,1,8,10368]{3,1,0,2:T(1,128)} %reshape_broadcast_in_dim.4), calls=%async_computation.4 | async-start | bytes 663552 | tf_op jit(solution)/shard_map/all_to_all | solution.py:39
  160.7 0.7 copy-start.13
  174.3 14.2 %all-to-all-start.5 = ((f32[1,8,1,10368]{3,2,0,1:T(1,128)}), f32[1,8,1,10368]{3,2,0,1:T(1,128)S(1)}, u32[]{:S(2)}, u32[]{:S(2)}) async-start(f32[1,8,1,10368]{3,2,0,1:T(1,128)} %copy.47), calls=%async_computation.5 | async-start | bytes 663552 | tf_op jit(solution)/shard_map/all_to_all | solution.py:38
  178.0 8.4 %copy-start.9 = (pred[576]{0:T(1024)(128)(4,1)S(1)}, pred[576]{0:T(1024)(128)(4,1)}, u32[]{:S(2)}) copy-start(pred[576]{0:T(1024)(128)(4,1)} %copy-done.8) | copy-start | bytes 1732
  178.0 8.4 %copy-start.11 = (pred[144]{0:T(512)(128)(4,1)S(1)}, pred[144]{0:T(512)(128)(4,1)}, u32[]{:S(2)}) copy-start(pred[144]{0:T(512)(128)(4,1)} %copy-done.10) | copy-start | bytes 436
  191.9 1.0 copy-start.3
where the time goes:
time: 195 us; the launch traced here: 194 us
  blocking collectives  95 us (49%)
  local copies, waits for them, and re-layouts  35.8 us (18%)
  starting transfers between devices  18.9 us (10%)
  waiting for transfers between devices  18.7 us (10%)
  other arithmetic  14.3 us (7%)
  matrix products  10.2 us (5%)
    all_gather x4, blocking collectives, commutator(): lax.all_gather(right_rows.astype(jnp.bfloat16), 'blk', axis=1, tiled=True)  32.9 us
    all_to_all x1, blocking collectives, through_mixing(): lax.all_to_all(shaped, 'chan', split_axis=2, concat_axis=1, tiled=True)  24.1 us
    all_to_all x1, blocking collectives, through_mixing(): lax.all_to_all(apply_fn(lax.all_to_all(shaped, 'chan', split_axis=2, conc...  20.8 us
    all_to_all x2, waiting for transfers between devices, through_mixing(): lax.all_to_all(shaped, 'chan', split_axis=2, concat_axis=1, tiled=True)  17.7 us
    all_to_all x2, starting transfers between devices, through_mixing(): lax.all_to_all(shaped, 'chan', split_axis=2, concat_axis=1, tiled=True)  11.5 us
    all_gather x1, blocking collectives, on_device(): lax.all_gather(gen_cross.astype(jnp.bfloat16), 'blk', axis=1, tiled=True)  8.82 us
    all_gather x1, blocking collectives, on_device(): lax.all_gather(generator.astype(jnp.bfloat16), 'blk', axis=1, tiled=True)  8.42 us
    all_to_all x2, starting transfers between devices, through_mixing(): lax.all_to_all(apply_fn(lax.all_to_all(shaped, 'chan', split_axis=2, conc...  7.39 us
  transfers between devices with their start and end apart: 4, of which 3 were waited for; matrix products, arithmetic and copies ran while one was open for 8% of the time, Pallas kernels for 0%

commit v1 on v0

v1 whole, which is shorter than its diff:
```python
import functools

import jax
import jax.numpy as jnp
from jax import lax
from jax.experimental import pallas as pl
from jax.experimental.pallas import tpu as pltpu
from jax.sharding import PartitionSpec as P

exact_mode = lax.Precision.HIGHEST
f32 = jnp.float32
bf16 = jnp.bfloat16
i16 = jnp.int16
LEVELS = 32760.0
STEP = 0.08664339756999316
TINY = 1e-30
HALF = 64


def vmem():
    return pl.BlockSpec(memory_space=pltpu.VMEM)


def smem():
    return pl.BlockSpec(memory_space=pltpu.SMEM)


class Plan:
    def __init__(self, rows, width, chan, blk):
        assert rows % 16 == 0 and width % 128 in (0, HALF) and width >= 128
        self.rows, self.width, self.chan, self.blk = rows, width, chan, blk
        self.full = width // 128
        self.tail = width % 128 != 0
        self.groups = rows // 8
        self.main = self.full * 128
        self.wide = self.main + (128 if self.tail else 0)
        self.packed = 2 * self.main + (128 if self.tail else 0)
        self.tiles = self.groups * self.full + (self.groups // 2 if self.tail else 0)
        self.slots = -(-self.tiles // chan)
        self.pair_rows = 16 * (self.slots + 1)
        self.single_rows = 16 * ((self.slots + 2) // 2)

    def load(self, ref, u):
        if u >= self.tiles:
            return jnp.zeros((8, 128), f32)
        if u < self.groups * self.full:
            g, j = divmod(u, self.full)
            return ref[8 * g : 8 * g + 8, 128 * j : 128 * j + 128]
        v = 16 * (u - self.groups * self.full)
        first = ref[v : v + 8, self.main : self.wide]
        second = pltpu.roll(ref[v + 8 : v + 16, self.main : self.wide], HALF, 1)
        return jnp.where(low_lanes((8, 128)), first, second)

    def store(self, ref, u, tile):
        if u >= self.tiles:
            return
        if u < self.groups * self.full:
            g, j = divmod(u, self.full)
            ref[8 * g : 8 * g + 8, 128 * j : 128 * j + 128] = tile
            return
        v = 16 * (u - self.groups * self.full)
        ref[v : v + 8, self.main : self.wide] = tile
        ref[v + 8 : v + 16, self.main : self.wide] = pltpu.roll(tile, HALF, 1)


def low_lanes(shape):
    return lax.broadcasted_iota(jnp.int32, shape, len(shape) - 1) < HALF


def exponent_of(peak):
    return jnp.floor(jnp.log(jnp.maximum(peak, TINY)) * (1.0 / STEP)) + 1.0


def to_int(value):
    return jnp.round(value).astype(jnp.int32).astype(i16)


def from_int(value):
    return value.astype(jnp.int32).astype(f32)


def pack_pair(plan, first_ref, second_ref, out_ref):
    for chunk in range(plan.chan):
        us = [chunk * plan.slots + p for p in range(plan.slots)]
        values = [jnp.concatenate([plan.load(first_ref, u), plan.load(second_ref, u)], axis=0) for u in us]
        peak = functools.reduce(jnp.maximum, [jnp.abs(v) for v in values])
        e = exponent_of(peak)
        up = jnp.exp(e * -STEP) * LEVELS
        for p, v in enumerate(values):
            out_ref[chunk, 16 * p : 16 * p + 16, :] = to_int(v * up)
        out_ref[chunk, 16 * plan.slots : 16 * plan.slots + 16, :] = to_int(e)


def unpack_pair(plan, in_ref, first_ref, second_ref):
    for chunk in range(plan.chan):
        e = from_int(in_ref[chunk, 16 * plan.slots : 16 * plan.slots + 16, :])
        down = jnp.exp(e * STEP) * (1.0 / LEVELS)
        for p in range(plan.slots):
            u = chunk * plan.slots + p
            if u < plan.tiles:
                v = from_int(in_ref[chunk, 16 * p : 16 * p + 16, :]) * down
                plan.store(first_ref, u, v[0:8])
                plan.store(second_ref, u, v[8:16])


def pack_single(plan, ref, out_ref):
    for chunk in range(plan.chan):
        us = [chunk * plan.slots + p for p in range(plan.slots)]
        values = [plan.load(ref, u) for u in us]
        peak = functools.reduce(jnp.maximum, [jnp.abs(v) for v in values])
        e = exponent_of(peak)
        up = jnp.exp(e * -STEP) * LEVELS
        scaled = [v * up for v in values] + [e]
        if len(scaled) % 2:
            scaled.append(e)
        for p in range(0, len(scaled), 2):
            out_ref[chunk, 8 * p : 8 * p + 16, :] = to_int(jnp.concatenate(scaled[p : p + 2], axis=0))


def single_exponent(plan, tile):
    at = 8 * plan.slots % 16
    return tile[at : at + 8]


def unpack_single(plan, in_ref, ref):
    last = plan.slots // 2
    for chunk in range(plan.chan):
        e = single_exponent(plan, from_int(in_ref[chunk, 16 * last : 16 * last + 16, :]))
        down = jnp.exp(e * STEP) * (1.0 / LEVELS)
        for p in range(0, plan.slots, 2):
            v = from_int(in_ref[chunk, 8 * p : 8 * p + 16, :])
            for q in range(2):
                u = chunk * plan.slots + p + q
                if p + q < plan.slots and u < plan.tiles:
                    plan.store(ref, u, v[8 * q : 8 * q + 8] * down)


def store_packed(plan, first, second, out_ref):
    m = plan.main
    out_ref[:, 0:m] = first[:, 0:m].astype(bf16)
    out_ref[:, m : 2 * m] = second[:, 0:m].astype(bf16)
    if plan.tail:
        a = first[:, m : plan.wide]
        b = pltpu.roll(second[:, m : plan.wide], HALF, 1)
        out_ref[:, 2 * m :] = jnp.where(low_lanes(a.shape), a, b).astype(bf16)


def assemble(plan, pieces, blk_ref, out_ref):
    for s, piece in enumerate(pieces):
        at = pl.multiple_of((blk_ref[0] ^ s) * plan.rows, 16)
        out_ref[pl.ds(at, plan.rows), :] = piece[...]


def dot(a, b):
    return jnp.dot(a, b, preferred_element_type=f32)


def product(plan, left, right_ref, second, main_ref, tail):
    m = plan.main
    at = m if second else 0
    main = dot(left, right_ref[:, at : at + m])
    if not plan.tail:
        return main, None
    last = dot(left, right_ref[:, 2 * m :])
    return main, (pltpu.roll(last, HALF, 1) if second else last)


def commute(plan, left, right_ref, right_second, other_left, other_ref, other_second, out_ref):
    a, a_tail = product(plan, left, right_ref, right_second, None, None)
    b, b_tail = product(plan, other_left, other_ref, other_second, None, None)
    out_ref[:, 0 : plan.main] = a - b
    if plan.tail:
        out_ref[:, plan.main : plan.wide] = a_tail - b_tail


def kernel_enter(plan, omega, ham, occ, size, blk, send, packed, left_gen, left_ham, gen_s, ham_s):
    shape = (plan.rows, plan.width)
    row = lax.broadcasted_iota(jnp.int32, shape, 0) + blk[0] * plan.rows
    col = lax.broadcasted_iota(jnp.int32, shape, 1)
    inside = (row < size[0]) & (col < size[0])
    gen = jnp.where(inside, omega[...], 0.0)
    start = jnp.where(inside, ham[...], 0.0)
    gen_s[:, 0 : plan.width] = gen
    ham_s[:, 0 : plan.width] = start
    left_gen[...] = (gen * occ[...]).astype(bf16)
    left_ham[...] = (start * occ[...]).astype(bf16)
    pack_pair(plan, gen_s, ham_s, send)
    store_packed(plan, gen_s, ham_s, packed)


def kernel_prepare(plan, column_map, occ, select, moved_occ):
    w = plan.width
    rows = lax.broadcasted_iota(jnp.int32, (w, w), 0)
    hot = (rows == column_map[...]).astype(f32).astype(bf16)
    select[...] = hot
    value = occ[...]
    high = value.astype(bf16)
    rest = value - high.astype(f32)
    middle = rest.astype(bf16)
    low = (rest - middle.astype(f32)).astype(bf16)
    total = jnp.zeros((8, w), f32)
    for part in (low, middle, high):
        total = total + lax.dot_general(
            jnp.broadcast_to(part.astype(f32), (8, w)).astype(bf16),
            hot,
            (((1,), (1,)), ((), ())),
            preferred_element_type=f32,
        )
    moved_occ[...] = total[0:1]


def kernel_unpack_cross(plan, recv, packed, gen, ham):
    unpack_pair(plan, recv, gen, ham)
    store_packed(plan, gen, ham, packed)


def moved_left(plan, value_ref, moved_occ, select):
    scaled = (value_ref[:, 0 : plan.width] * moved_occ[...]).astype(bf16)
    return dot(scaled, select[...]).astype(bf16)


def kernel_cross_left(plan, gen, ham, moved_occ, select, left_gen, left_ham):
    left_gen[...] = moved_left(plan, gen, moved_occ, select)
    left_ham[...] = moved_left(plan, ham, moved_occ, select)


def kernel_first_pair(plan, left_gen, left_ham, blk, *refs):
    pieces, (right, first) = refs[: plan.blk], refs[plan.blk :]
    assemble(plan, pieces, blk, right)
    commute(plan, left_gen[...], right, True, left_ham[...], right, False, first)


def kernel_first_cross(plan, left_gen, left_ham, first, blk, *refs):
    pieces, (right, send, cross_s) = refs[: plan.blk], refs[plan.blk :]
    assemble(plan, pieces, blk, right)
    commute(plan, left_gen[...], right, True, left_ham[...], right, False, cross_s)
    pack_pair(plan, cross_s, first, send)


def kernel_unpack_eta(plan, recv, first, occ, packed, eta, cross, left_eta):
    unpack_pair(plan, recv, eta, cross)
    eta[...] = eta[...] + first[...]
    left_eta[...] = (eta[:, 0 : plan.width] * occ[...]).astype(bf16)
    store_packed(plan, cross, eta, packed)


def kernel_eta_left(plan, cross, moved_occ, select, left_cross):
    left_cross[...] = moved_left(plan, cross, moved_occ, select)


def kernel_second_cross(plan, left_gen, left_eta, right_cross, blk, *refs):
    pieces, (right, send, cross_s) = refs[: plan.blk], refs[plan.blk :]
    assemble(plan, pieces, blk, right)
    commute(plan, left_gen[...], right, False, left_eta[...], right_cross, False, cross_s)
    pack_single(plan, cross_s, send)


def kernel_second_pair(plan, left_gen, left_eta, right_eta, right_gen, second):
    commute(plan, left_gen[...], right_eta, True, left_eta[...], right_gen, False, second)


def kernel_finish(plan, recv, ham, eta, second, size, blk, out, back_s):
    unpack_single(plan, recv, back_s)
    w = plan.width
    shape = (plan.rows, w)
    row = lax.broadcasted_iota(jnp.int32, shape, 0) + blk[0] * plan.rows
    col = lax.broadcasted_iota(jnp.int32, shape, 1)
    inside = (row < size[0]) & (col < size[0])
    total = ham[...] + eta[:, 0:w] + 0.5 * (second[:, 0:w] + back_s[:, 0:w])
    out[...] = jnp.where(inside, total, 0.0)


def mixed(mixing, values, transposed):
    n = len(values)
    out = []
    for k in range(n):
        terms = [values[c] * (mixing[c, k] if transposed else mixing[k, c]) for c in range(n)]
        out.append(functools.reduce(jnp.add, terms))
    return out


def both_of(mixing, values):
    restored = mixed(mixing, [v[0:8] for v in values], True)
    crossed = mixed(mixing, [v[8:16] + r for v, r in zip(values, restored)], False)
    return [jnp.concatenate(pair, axis=0) for pair in zip(restored, crossed)]


def kernel_mix(plan, kind, mixing, recv, send, kept):
    n = plan.chan
    slots = plan.slots
    if kind == "back":
        tiles = plan.single_rows // 16
        e_all = [single_exponent(plan, from_int(recv[c, 16 * (slots // 2) : 16 * (slots // 2) + 16, :])) for c in range(n)]
        down = [jnp.exp(e * STEP) * (1.0 / LEVELS) for e in e_all]
        down = [jnp.concatenate([d, d], axis=0) for d in down]
        odd = slots % 2
    else:
        tiles = slots
        down = [jnp.exp(from_int(recv[c, 16 * slots : 16 * slots + 16, :]) * STEP) * (1.0 / LEVELS) for c in range(n)]
    peak = [jnp.zeros((16, 128), f32) for _ in range(n)]
    for p in range(tiles if kind != "back" else (slots + 1) // 2):
        values = [from_int(recv[c, 16 * p : 16 * p + 16, :]) * down[c] for c in range(n)]
        if kind == "cross":
            result = mixed(mixing, values, False)
        elif kind == "both":
            result = both_of(mixing, values)
        else:
            result = mixed(mixing, values, True)
            if odd and p == (slots + 1) // 2 - 1:
                result = [jnp.concatenate([r[0:8], jnp.zeros((8, 128), f32)], axis=0) for r in result]
        for k in range(n):
            kept[k, 16 * p : 16 * p + 16, :] = result[k]
            peak[k] = jnp.maximum(peak[k], jnp.abs(result[k]))
    for k in range(n):
        top = peak[k]
        if kind == "back":
            top = jnp.maximum(top[0:8], top[8:16])
            top = jnp.concatenate([top, top], axis=0)
        e = exponent_of(top)
        up = jnp.exp(e * -STEP) * LEVELS
        if kind != "back":
            for p in range(slots):
                send[k, 16 * p : 16 * p + 16, :] = to_int(kept[k, 16 * p : 16 * p + 16, :] * up)
            send[k, 16 * slots : 16 * slots + 16, :] = to_int(e)
        else:
            for p in range(tiles):
                if 2 * p + 1 < slots:
                    value = kept[k, 16 * p : 16 * p + 16, :] * up
                elif 2 * p < slots:
                    value = jnp.concatenate([kept[k, 16 * p : 16 * p + 8, :] * up[0:8], e[0:8]], axis=0)
                else:
                    value = e
                send[k, 16 * p : 16 * p + 16, :] = to_int(value)


def plain_mix(plan, kind, mixing, recv):
    n, slots = plan.chan, plan.slots

    def mix(spec, value):
        return jnp.einsum(spec, mixing, value, precision=exact_mode, preferred_element_type=f32)

    raw = recv.astype(jnp.int32).astype(f32)
    if kind == "back":
        e = raw[:, 8 * slots : 8 * slots + 8]
        body = raw[:, 0 : 8 * slots].reshape(n, slots, 8, 128)
    else:
        e = raw[:, 16 * slots : 16 * slots + 16]
        body = raw[:, 0 : 16 * slots].reshape(n, slots, 16, 128)
    body = body * (jnp.exp(e * STEP) * (1.0 / LEVELS))[:, None]
    if kind == "cross":
        result = mix("kc,cpsl->kpsl", body)
    elif kind == "both":
        restored = mix("ck,cpsl->kpsl", body[:, :, 0:8])
        crossed = mix("kc,cpsl->kpsl", body[:, :, 8:16] + restored)
        result = jnp.concatenate([restored, crossed], axis=2)
    else:
        result = mix("ck,cpsl->kpsl", body)
    e = exponent_of(jnp.max(jnp.abs(result), axis=1))
    scaled = result * (jnp.exp(e * -STEP) * LEVELS)[:, None]
    out = jnp.concatenate([scaled.reshape(n, -1, 128), e], axis=1)
    out = jnp.pad(out, ((0, 0), (0, recv.shape[1] - out.shape[1]), (0, 0)))
    return to_int(out)


def call(body, plan, outs, specs, scratch=()):
    return pl.pallas_call(
        functools.partial(body, plan),
        out_shape=tuple(jax.ShapeDtypeStruct(s, d) for s, d in outs),
        in_specs=specs,
        out_specs=tuple(vmem() for _ in outs),
        scratch_shapes=tuple(pltpu.VMEM(s, d) for s, d in scratch),
        name=body.__name__,
    )


def mix_call(plan, kind, mixing, recv):
    if plan.chan > 16:
        return plain_mix(plan, kind, mixing, recv)
    rows = recv.shape[1]
    return pl.pallas_call(
        functools.partial(kernel_mix, plan, kind),
        out_shape=jax.ShapeDtypeStruct(recv.shape, i16),
        in_specs=[smem(), vmem()],
        out_specs=vmem(),
        scratch_shapes=(pltpu.VMEM((plan.chan, rows, 128), f32),),
        name="mix_" + kind,
    )(mixing, recv)


def mixing_matrix(jlabel, family, sixj):
    levels = sixj.shape[0]
    one_hot = (jlabel[:, None] == jnp.arange(levels, dtype=jnp.int32)[None, :]).astype(f32)
    picked = jnp.dot(one_hot, sixj, precision=exact_mode, preferred_element_type=f32)
    picked = jnp.dot(picked, one_hot.T, precision=exact_mode, preferred_element_type=f32)
    kindred = (family[:, None] == family[None, :]).astype(f32)
    return picked * kindred


def gather_rows(value, size):
    pieces = {0: value}
    bit = size // 2
    while bit:
        for s, piece in list(pieces.items()):
            pieces[s ^ bit] = lax.ppermute(piece, "blk", [(b, b ^ bit) for b in range(size)])
        bit //= 2
    return [pieces[s] for s in range(size)]


def exchange(value):
    return lax.all_to_all(value, "chan", 0, 0, tiled=True)


def on_device(omega, hamiltonian, pair_occ, cross_occ, block_size, jlabel, family, sixj, column_map):
    channels_here, rows, width = omega.shape
    assert channels_here == 1
    chan, blk = lax.axis_size("chan"), lax.axis_size("blk")
    assert blk & (blk - 1) == 0
    plan = Plan(rows, width, chan, blk)
    omega, ham = omega[0], hamiltonian[0]
    blk_index = lax.axis_index("blk").astype(jnp.int32).reshape(1)
    mixing = mixing_matrix(jlabel, family, sixj)
    pair = ((chan, plan.pair_rows, 128), i16)
    single = ((chan, plan.single_rows, 128), i16)
    packed = ((rows, plan.packed), bf16)
    left = ((rows, width), bf16)
    wide = ((rows, plan.wide), f32)
    right = ((rows * blk, plan.packed), bf16)

    send, pair_rows, left_gen, left_ham = call(
        kernel_enter, plan, [pair, packed, left, left], [vmem(), vmem(), vmem(), smem(), smem()], [wide, wide]
    )(omega, ham, pair_occ, block_size, blk_index)
    select, moved_occ = call(kernel_prepare, plan, [((width, width), bf16), ((1, width), f32)], [vmem(), vmem()])(
        column_map.reshape(1, width), cross_occ
    )
    recv = exchange(send)
    pair_pieces = gather_rows(pair_rows, blk)
    recv = exchange(mix_call(plan, "cross", mixing, recv))
    cross_rows, gen_cross, ham_cross = call(kernel_unpack_cross, plan, [packed, wide, wide], [vmem()])(recv)
    cross_pieces = gather_rows(cross_rows, blk)
    cross_gen_left, cross_ham_left = call(kernel_cross_left, plan, [left, left], [vmem()] * 4)(
        gen_cross, ham_cross, moved_occ, select
    )
    pair_right, first = call(kernel_first_pair, plan, [right, wide], [vmem(), vmem(), smem()] + [vmem()] * blk)(
        left_gen, left_ham, blk_index, *pair_pieces
    )
    cross_right, send = call(
        kernel_first_cross, plan, [right, pair], [vmem(), vmem(), vmem(), smem()] + [vmem()] * blk, [wide]
    )(cross_gen_left, cross_ham_left, first, blk_index, *cross_pieces)
    recv = exchange(mix_call(plan, "both", mixing, exchange(send)))
    eta_rows, eta, eta_cross, left_eta = call(kernel_unpack_eta, plan, [packed, wide, wide, left], [vmem()] * 3)(
        recv, first, pair_occ
    )
    eta_pieces = gather_rows(eta_rows, blk)
    (cross_eta_left,) = call(kernel_eta_left, plan, [left], [vmem()] * 3)(eta_cross, moved_occ, select)
    eta_right, send = call(
        kernel_second_cross, plan, [right, single], [vmem(), vmem(), vmem(), smem()] + [vmem()] * blk, [wide]
    )(cross_gen_left, cross_eta_left, cross_right, blk_index, *eta_pieces)
    (second,) = call(kernel_second_pair, plan, [wide], [vmem()] * 4)(left_gen, left_eta, eta_right, pair_right)
    recv = exchange(mix_call(plan, "back", mixing, exchange(send)))
    (out,) = call(kernel_finish, plan, [((rows, width), f32)], [vmem()] * 4 + [smem(), smem()], [wide])(
        recv, ham, eta, second, block_size, blk_index
    )
    return out[None]


def solution(mesh):
    in_specs = (
        P("chan", "blk", None),
        P("chan", "blk", None),
        P("chan", None),
        P("chan", None),
        P("chan"),
        P(),
        P(),
        P(),
        P(),
    )
    out_specs = P("chan", "blk", None)
    return jax.shard_map(
        on_device, mesh=mesh, in_specs=in_specs, out_specs=out_specs, check_vma=False
    )
```

time: 195 us -> 147 us (0.75)
  blocking collectives: 95 us -> 48.1 us
  Pallas kernels: 0 us -> 35.1 us
  local copies, waits for them, and re-layouts: 35.8 us -> 5.31 us
  waiting for transfers between devices: 18.7 us -> 36.3 us
  other arithmetic: 14.3 us -> 0 us
  matrix products: 10.2 us -> 0.98 us
    all_gather x6 -> x0, blocking collectives: 50.2 us -> none  [the longest x4 32.9 us: commutator(): lax.all_gather(right_rows.astype(jnp.bfloat16), 'blk', axis=1, tiled=True)]
    pallas_call x0 -> x14, Pallas kernels: none -> 35.1 us  [the longest x3 6.8 us: mix_call(): pl.pallas_call(functools.partial(kernel_mix, plan, kind), out_shape=jax.S...]
    gather x10 -> x0, local copies, waits for them, and re-layouts: 13.6 us -> none  [the longest x2 4.11 us: on_device(): first_pp[:, :, column_map]]
    ppermute x0 -> x9, waiting for transfers between devices: none -> 11 us  [gather_rows(): lax.ppermute(piece, 'blk', [(b, b ^ bit) for b in range(size)])]
    dot_general x14 -> x2, matrix products: 10.2 us -> 0.98 us  [the longest x1 0.8 us: mixing_matrix(): jnp.dot(picked, one_hot.T, precision=exact_mode, preferred_element_type=f32)]
    another operation x10 -> x0, local copies, waits for them, and re-layouts: 6.88 us -> none  [the longest x3 2.49 us: on_device(): jnp.stack([first_pp[:, :, column_map], first_cc])]
    convert_element_type x4 -> x0, other arithmetic: 6.73 us -> none  [the longest x1 4.08 us: on_device(): gen_cross.astype(jnp.bfloat16)]
    all_to_all x4 -> x3, waiting for transfers between devices: 18.7 us -> 25.2 us  [exchange(): return lax.all_to_all(value, 'chan', 0, 0, tiled=True)]
  transfers between devices with their start and end apart: 4 -> 12, of which waited for: 3 -> 5; matrix products, arithmetic and copies ran while one was open for 8% -> 1% of each run, Pallas kernels for 0% -> 10%
where the time goes in v1:
time: 147 us; the launch traced here: 146 us
  blocking collectives  48.1 us (33%)
  waiting for transfers between devices  36.3 us (25%)
  Pallas kernels  35.1 us (24%)
  starting transfers between devices  19.7 us (13%)
  local copies, waits for them, and re-layouts  5.31 us (4%)
    all_to_all x3, blocking collectives, exchange(): return lax.all_to_all(value, 'chan', 0, 0, tiled=True)  48.1 us
    all_to_all x3, waiting for transfers between devices, exchange(): return lax.all_to_all(value, 'chan', 0, 0, tiled=True)  25.2 us
    all_to_all x3, starting transfers between devices, exchange(): return lax.all_to_all(value, 'chan', 0, 0, tiled=True)  14.5 us
    ppermute x9, waiting for transfers between devices, gather_rows(): lax.ppermute(piece, 'blk', [(b, b ^ bit) for b in range(size)])  11 us
    pallas_call x3, Pallas kernels, mix_call(): pl.pallas_call(functools.partial(kernel_mix, plan, kind), out_shape=jax.S...  6.8 us
    ppermute x9, starting transfers between devices, gather_rows(): lax.ppermute(piece, 'blk', [(b, b ^ bit) for b in range(size)])  5.21 us
    unnamed x34, local copies, waits for them, and re-layouts  4.66 us
    pallas_call x1, Pallas kernels, on_device(): call(kernel_second_cross, plan, [right, single], [vmem(), vmem(), vmem(),...  3.23 us
  transfers between devices with their start and end apart: 12, of which 5 were waited for; matrix products, arithmetic and copies ran while one was open for 1% of the time, Pallas kernels for 10%

profile of v1, /device:TPU:0, one launch (start us, length us, event | category | flops | bytes accessed | tf_op | source)
XLA Modules:
  0.0 146.2 jit_solution(16927118803490378228)
XLA Ops:
  0.7 2.3 %kernel_enter.1 = (s16[8,192,128]{2,1,0:T(8,128)(2,1)}, bf16[144,1152]{1,0:T(8,128)(2,1)}, bf16[144,576]{1,0:T(8,128)(2,1)}, bf16[144,576]{1,0:T(8,128)(2,1)}) custom-call(f32[144,576]{1,0:T(8,128)} %bitcast.8, f32[144,576]{1,0:T(8,128)} %bitcast.6, f32[1,576]{1,0:T(1,128)} %occ.5, s32[1]{0:T(128)S(6)} %copy.10.size, s32[1]{0:T(128)} %bitcast.2.blk), custom_call_target="tpu_custom_call" | custom-call | tf_op jit(solution)/shard_map/kernel_enter/pallas_call | solution.py:429
  3.0 7.4 %all-to-all-start = ((s16[8,192,128]{2,1,0:T(8,128)(2,1)}), s16[8,192,128]{2,1,0:T(8,128)(2,1)S(1)}, u32[]{:S(2)}, u32[]{:S(2)}) async-start(s16[8,192,128]{2,1,0:T(8,128)(2,1)} %get-tuple-element.26), calls=%async_computation | async-start | bytes 786432 | tf_op jit(solution)/shard_map/all_to_all | solution.py:410
  10.5 0.2 fusion
  10.6 0.8 convolution_select_fusion.mixing
  11.4 10.7 %all-to-all-done.recv = s16[8,192,128]{2,1,0:T(8,128)(2,1)S(1)} async-done(((s16[8,192,128]{2,1,0:T(8,128)(2,1)}), s16[8,192,128]{2,1,0:T(8,128)(2,1)S(1)}, u32[]{:S(2)}, u32[]{:S(2)}) %all-to-all-start) | async-done | bytes 393248 | tf_op jit(solution)/shard_map/all_to_all | solution.py:410
  22.1 0.8 copy-done.2
  22.9 2.4 %mix_cross.1 = s16[8,192,128]{2,1,0:T(8,128)(2,1)} custom-call(f32[8,8]{1,0:T(8,128)} %convolution_select_fusion.mixing, s16[8,192,128]{2,1,0:T(8,128)(2,1)} %copy-done.2), custom_call_target="tpu_custom_call" | custom-call | tf_op jit(solution)/shard_map/mix_cross/pallas_call | solution.py:380
  25.3 3.6 %all-to-all-start.1 = ((s16[8,192,128]{2,1,0:T(8,128)(2,1)}), s16[8,192,128]{2,1,0:T(8,128)(2,1)S(1)}, u32[]{:S(2)}, u32[]{:S(2)}) async-start(s16[8,192,128]{2,1,0:T(8,128)(2,1)} %mix_cross.1), calls=%async_computation.1 | async-start | bytes 786432 | tf_op jit(solution)/shard_map/all_to_all | solution.py:410
  28.9 1.6 %collective-permute-start.1 = (bf16[144,1152]{1,0:T(8,128)(2,1)S(1)}, bf16[144,1152]{1,0:T(8,128)(2,1)S(1)}, u32[]{:S(2)}, u32[]{:S(2)}) collective-permute-start(bf16[144,1152]{1,0:T(8,128)(2,1)S(1)} %copy-done.10), channel_id=1, source_target_pairs={{0,2},{1,3},{2,0},{3,1},{4,6},{5,7},{6,4},{7,5},{8,10},{9,11},{10,... | collective-permute-start | bytes 995336 | tf_op jit(solution)/shard_map/ppermute | solution.py:404
  30.5 10.0 %all-to-all-done.1.recv = s16[8,192,128]{2,1,0:T(8,128)(2,1)S(1)} async-done(((s16[8,192,128]{2,1,0:T(8,128)(2,1)}), s16[8,192,128]{2,1,0:T(8,128)(2,1)S(1)}, u32[]{:S(2)}, u32[]{:S(2)}) %all-to-all-start.1) | async-done | bytes 393248 | tf_op jit(solution)/shard_map/all_to_all | solution.py:410
  40.5 0.8 copy-done.1
  41.3 2.1 %kernel_unpack_cross.1 = (bf16[144,1152]{1,0:T(8,128)(2,1)}, f32[144,640]{1,0:T(8,128)}, f32[144,640]{1,0:T(8,128)}) custom-call(s16[8,192,128]{2,1,0:T(8,128)(2,1)} %copy-done.1), custom_call_target="tpu_custom_call" | custom-call | tf_op jit(solution)/shard_map/kernel_unpack_cross/pallas_call | solution.py:438
  43.4 1.5 %collective-permute-start.4 = (bf16[144,1152]{1,0:T(8,128)(2,1)}, bf16[144,1152]{1,0:T(8,128)(2,1)S(1)}, u32[]{:S(2)}, u32[]{:S(2)}) collective-permute-start(bf16[144,1152]{1,0:T(8,128)(2,1)} %get-tuple-element.37.refs_0_), channel_id=1, source_target_pairs={{0,2},{1,3},{2,0},{3,1},{4,6},{5,7},{6,4},{7,5},{8,10},{9,11},{10,... | collective-permute-start | bytes 995336 | tf_op jit(solution)/shard_map/ppermute | solution.py:404
  44.9 0.0 collective-permute-start
  44.9 0.0 collective-permute-done.1.refs_2_
  44.9 0.5 collective-permute-start.2
  45.4 0.1 collective-permute-start.3
  45.5 5.2 %collective-permute-done.4.refs_2_ = bf16[144,1152]{1,0:T(8,128)(2,1)S(1)} collective-permute-done((bf16[144,1152]{1,0:T(8,128)(2,1)}, bf16[144,1152]{1,0:T(8,128)(2,1)S(1)}, u32[]{:S(2)}, u32[]{:S(2)}) %collective-permute-start.4) | collective-permute-done | bytes 331808 | tf_op jit(solution)/shard_map/ppermute | solution.py:404
  50.7 0.6 reshape.10.column_map
  51.4 2.1 %kernel_prepare.1 = (bf16[576,576]{1,0:T(8,128)(2,1)}, f32[1,576]{1,0:T(1,128)}) custom-call(s32[1,576]{1,0:T(1,128)} %reshape.10.column_map, f32[1,576]{1,0:T(1,128)} %occ.4), custom_call_target="tpu_custom_call" | custom-call | tf_op jit(solution)/shard_map/kernel_prepare/pallas_call | solution.py:432
  53.5 0.0 collective-permute-done.refs_1_
  53.5 0.7 copy-done.12
  54.2 0.1 copy-done.13
  54.3 2.8 %kernel_first_pair.1 = (bf16[576,1152]{1,0:T(8,128)(2,1)}, f32[144,640]{1,0:T(8,128)}) custom-call(bf16[144,576]{1,0:T(8,128)(2,1)} %get-tuple-element.33.left_gen, bf16[144,576]{1,0:T(8,128)(2,1)} %get-tuple-element.34.left_ham, s32[1]{0:T(128)} %bitcast.2.blk, bf16[144,1152]{1,0:T(8,128)(2,1)} %get-tuple-element.35.refs_0_, bf16[144,1152]{1,0:T(8,128)(2,1)} %copy-done.12, ...), custom_call_target="tpu_custom_call" | custom-call | tf_op jit(solution)/shard_map/kernel_first_pair/pallas_call | solution.py:443
  57.1 2.5 %kernel_cross_left.1 = (bf16[144,576]{1,0:T(8,128)(2,1)}, bf16[144,576]{1,0:T(8,128)(2,1)}) custom-call(f32[144,640]{1,0:T(8,128)} %get-tuple-element.27.gen, f32[144,640]{1,0:T(8,128)} %get-tuple-element.28.ham, f32[1,576]{1,0:T(1,128)} %get-tuple-element.29.moved_occ, bf16[576,576]{1,0:T(8,128)(2,1)} %get-tuple-element.30.select), custom_call_target="tpu_custom_call" | custom-call | tf_op jit(solution)/shard_map/kernel_cross_left/pallas_call | solution.py:440
  59.7 0.0 collective-permute-done.3.refs_1_
  59.7 0.0 collective-permute-done.5.refs_3_
  59.7 0.7 copy-done.5
  60.4 0.1 copy-done.6
  60.5 3.0 %kernel_first_cross.1 = (bf16[576,1152]{1,0:T(8,128)(2,1)}, s16[8,192,128]{2,1,0:T(8,128)(2,1)}) custom-call(bf16[144,576]{1,0:T(8,128)(2,1)} %get-tuple-element.31.left_gen, bf16[144,576]{1,0:T(8,128)(2,1)} %get-tuple-element.32.left_ham, f32[144,640]{1,0:T(8,128)} %get-tuple-element.36.first, s32[1]{0:T(128)} %bitcast.2.blk, ...), custom_call_target="tpu_custom_call" | custom-call | tf_op jit(solution)/shard_map/kernel_first_cross/pallas_call | solution.py:446
  63.5 18.6 %all_to_all.30.recv = s16[8,192,128]{2,1,0:T(8,128)(2,1)} all-to-all(s16[8,192,128]{2,1,0:T(8,128)(2,1)} %get-tuple-element.38), channel_id=1, replica_groups=mesh['chan'=8,'blk'=4] {'chan'}, dimensions={0} | all-to-all | bytes 786432 | tf_op jit(solution)/shard_map/all_to_all | solution.py:410
  82.2 2.5 %mix_both.1 = s16[8,192,128]{2,1,0:T(8,128)(2,1)} custom-call(f32[8,8]{1,0:T(8,128)} %convolution_select_fusion.mixing, s16[8,192,128]{2,1,0:T(8,128)(2,1)} %all_to_all.30.recv), custom_call_target="tpu_custom_call" | custom-call | tf_op jit(solution)/shard_map/mix_both/pallas_call | solution.py:380
  84.7 15.6 %all_to_all.31.recv = s16[8,192,128]{2,1,0:T(8,128)(2,1)} all-to-all(s16[8,192,128]{2,1,0:T(8,128)(2,1)} %mix_both.1), channel_id=1, replica_groups=mesh['chan'=8,'blk'=4] {'chan'}, dimensions={0} | all-to-all | bytes 786432 | tf_op jit(solution)/shard_map/all_to_all | solution.py:410
  100.3 2.4 %kernel_unpack_eta.1 = (bf16[144,1152]{1,0:T(8,128)(2,1)}, f32[144,640]{1,0:T(8,128)}, f32[144,640]{1,0:T(8,128)}, bf16[144,576]{1,0:T(8,128)(2,1)}) custom-call(s16[8,192,128]{2,1,0:T(8,128)(2,1)} %all_to_all.31.recv, f32[144,640]{1,0:T(8,128)} %get-tuple-element.36.first, f32[1,576]{1,0:T(1,128)} %occ.5), custom_call_target="tpu_custom_call" | custom-call | tf_op jit(solution)/shard_map/kernel_unpack_eta/pallas_call | solution.py:450
  102.7 1.5 %collective-permute-start.7 = (bf16[144,1152]{1,0:T(8,128)(2,1)}, bf16[144,1152]{1,0:T(8,128)(2,1)S(1)}, u32[]{:S(2)}, u32[]{:S(2)}) collective-permute-start(bf16[144,1152]{1,0:T(8,128)(2,1)} %get-tuple-element.41.refs_0_), channel_id=1, source_target_pairs={{0,2},{1,3},{2,0},{3,1},{4,6},{5,7},{6,4},{7,5},{8,10},{9,11},{10,... | collective-permute-start | bytes 995336 | tf_op jit(solution)/shard_map/ppermute | solution.py:404
  104.2 5.8 %collective-permute-done.7.refs_2_ = bf16[144,1152]{1,0:T(8,128)(2,1)S(1)} collective-permute-done((bf16[144,1152]{1,0:T(8,128)(2,1)}, bf16[144,1152]{1,0:T(8,128)(2,1)S(1)}, u32[]{:S(2)}, u32[]{:S(2)}) %collective-permute-start.7) | collective-permute-done | bytes 331808 | tf_op jit(solution)/shard_map/ppermute | solution.py:404
  110.0 0.0 collective-permute-start.8
  110.0 2.4 %kernel_eta_left.1.left_eta = bf16[144,576]{1,0:T(8,128)(2,1)} custom-call(f32[144,640]{1,0:T(8,128)} %get-tuple-element.39.cross, f32[1,576]{1,0:T(1,128)} %get-tuple-element.29.moved_occ, bf16[576,576]{1,0:T(8,128)(2,1)} %get-tuple-element.30.select), custom_call_target="tpu_custom_call" | custom-call | tf_op jit(solution)/shard_map/kernel_eta_left/pallas_call | solution.py:454
  112.4 0.7 copy-done.8
  113.1 0.1 copy-done.9
  113.2 3.2 %kernel_second_cross.1 = (bf16[576,1152]{1,0:T(8,128)(2,1)}, s16[8,96,128]{2,1,0:T(8,128)(2,1)}) custom-call(bf16[144,576]{1,0:T(8,128)(2,1)} %get-tuple-element.31.left_gen, bf16[144,576]{1,0:T(8,128)(2,1)} %kernel_eta_left.1.left_eta, bf16[576,1152]{1,0:T(8,128)(2,1)} %get-tuple-element.40.right_cross, s32[1]{0:T(128)} %bitcast.2.blk, ...), custom_call_target="tpu_custom_call" | custom-call | tf_op jit(solution)/shard_map/kernel_second_cross/pallas_call | solution.py:455
  116.4 13.8 %all_to_all.32.recv = s16[8,96,128]{2,1,0:T(8,128)(2,1)} all-to-all(s16[8,96,128]{2,1,0:T(8,128)(2,1)} %get-tuple-element.42), channel_id=1, replica_groups=mesh['chan'=8,'blk'=4] {'chan'}, dimensions={0} | all-to-all | bytes 393216 | tf_op jit(solution)/shard_map/all_to_all | solution.py:410
  130.3 1.9 %mix_back.1 = s16[8,96,128]{2,1,0:T(8,128)(2,1)} custom-call(f32[8,8]{1,0:T(8,128)} %convolution_select_fusion.mixing, s16[8,96,128]{2,1,0:T(8,128)(2,1)} %all_to_all.32.recv), custom_call_target="tpu_custom_call" | custom-call | tf_op jit(solution)/shard_map/mix_back/pallas_call | solution.py:380
  132.2 3.4 %all-to-all-start.5 = ((s16[8,96,128]{2,1,0:T(8,128)(2,1)}), s16[8,96,128]{2,1,0:T(8,128)(2,1)S(1)}, u32[]{:S(2)}, u32[]{:S(2)}) async-start(s16[8,96,128]{2,1,0:T(8,128)(2,1)} %mix_back.1), calls=%async_computation.5 | async-start | bytes 393216 | tf_op jit(solution)/shard_map/all_to_all | solution.py:410
  135.6 3.2 %kernel_second_pair.1.second = f32[144,640]{1,0:T(8,128)} custom-call(bf16[144,576]{1,0:T(8,128)(2,1)} %get-tuple-element.33.left_gen, bf16[144,576]{1,0:T(8,128)(2,1)} %get-tuple-element.44.left_eta, bf16[576,1152]{1,0:T(8,128)(2,1)} %get-tuple-element.45.right_eta, bf16[576,1152]{1,0:T(8,128)(2,1)} %get-tuple-element.46.right_gen), custom_call_target="tpu_custom_call" | custom-call | tf_op jit(solution)/shard_map/kernel_second_pair/pallas_call | solution.py:458
  138.8 4.5 %all-to-all-done.5.recv = s16[8,96,128]{2,1,0:T(8,128)(2,1)S(1)} async-done(((s16[8,96,128]{2,1,0:T(8,128)(2,1)}), s16[8,96,128]{2,1,0:T(8,128)(2,1)S(1)}, u32[]{:S(2)}, u32[]{:S(2)}) %all-to-all-start.5) | async-done | bytes 196640 | tf_op jit(solution)/shard_map/all_to_all | solution.py:410
  143.3 0.7 copy-done.3
  144.0 2.2 %kernel_finish.1 = f32[144,576]{1,0:T(8,128)} custom-call(s16[8,96,128]{2,1,0:T(8,128)(2,1)} %copy-done.3, f32[144,576]{1,0:T(8,128)} %bitcast.7, f32[144,640]{1,0:T(8,128)} %get-tuple-element.43.eta, f32[144,640]{1,0:T(8,128)} %kernel_second_pair.1.second, s32[1]{0:T(128)S(6)} %copy.10.size, s32[1]{0:T(128)} %bitcast.2.blk), custom_call_target="tpu_custom_call" | custom-call | tf_op jit(solution)/shard_map/kernel_finish/pallas_call | solution.py:460
  (30 shorter events, 0.1 us)
Async XLA Ops:
  0.0 10.4 %copy-start = (f32[8,8]{1,0:T(8,128)S(1)}, f32[8,8]{1,0:T(8,128)}, u32[]{:S(2)}) copy-start(f32[8,8]{1,0:T(8,128)} %param.16) | copy-start | bytes 772
  0.0 10.4 %copy-start.15 = (s32[8]{0:T(128)S(1)}, s32[8]{0:T(128)}, u32[]{:S(2)}) copy-start(s32[8]{0:T(128)} %param.14) | copy-start | bytes 100
  0.0 10.6 %copy-start.16 = (s32[8]{0:T(128)S(1)}, s32[8]{0:T(128)}, u32[]{:S(2)}) copy-start(s32[8]{0:T(128)} %param.15) | copy-start | bytes 100
  3.0 25.9 %copy-start.10 = (bf16[144,1152]{1,0:T(8,128)(2,1)S(1)}, bf16[144,1152]{1,0:T(8,128)(2,1)}, u32[]{:S(2)}) copy-start(bf16[144,1152]{1,0:T(8,128)(2,1)} %get-tuple-element.35.refs_0_) | copy-start | bytes 995332
  3.0 47.7 %copy-start.14 = (s32[576]{0:T(1024)S(1)}, s32[576]{0:T(1024)}, u32[]{:S(2)}) copy-start(s32[576]{0:T(1024)} %param.17) | copy-start | bytes 6916
  3.0 19.1 %all-to-all-start = ((s16[8,192,128]{2,1,0:T(8,128)(2,1)}), s16[8,192,128]{2,1,0:T(8,128)(2,1)S(1)}, u32[]{:S(2)}, u32[]{:S(2)}) async-start(s16[8,192,128]{2,1,0:T(8,128)(2,1)} %get-tuple-element.26), calls=%async_computation | async-start | bytes 786432 | tf_op jit(solution)/shard_map/all_to_all | solution.py:410
  22.1 0.8 copy-start.2
  25.3 15.3 %all-to-all-start.1 = ((s16[8,192,128]{2,1,0:T(8,128)(2,1)}), s16[8,192,128]{2,1,0:T(8,128)(2,1)S(1)}, u32[]{:S(2)}, u32[]{:S(2)}) async-start(s16[8,192,128]{2,1,0:T(8,128)(2,1)} %mix_cross.1), calls=%async_computation.1 | async-start | bytes 786432 | tf_op jit(solution)/shard_map/all_to_all | solution.py:410
  28.9 16.0 %collective-permute-start.1 = (bf16[144,1152]{1,0:T(8,128)(2,1)S(1)}, bf16[144,1152]{1,0:T(8,128)(2,1)S(1)}, u32[]{:S(2)}, u32[]{:S(2)}) collective-permute-start(bf16[144,1152]{1,0:T(8,128)(2,1)S(1)} %copy-done.10), channel_id=1, source_target_pairs={{0,2},{1,3},{2,0},{3,1},{4,6},{5,7},{6,4},{7,5},{8,10},{9,11},{10,... | collective-permute-start | bytes 995336 | tf_op jit(solution)/shard_map/ppermute | solution.py:404
  40.5 0.8 copy-start.1
  43.4 7.3 %collective-permute-start.4 = (bf16[144,1152]{1,0:T(8,128)(2,1)}, bf16[144,1152]{1,0:T(8,128)(2,1)S(1)}, u32[]{:S(2)}, u32[]{:S(2)}) collective-permute-start(bf16[144,1152]{1,0:T(8,128)(2,1)} %get-tuple-element.37.refs_0_), channel_id=1, source_target_pairs={{0,2},{1,3},{2,0},{3,1},{4,6},{5,7},{6,4},{7,5},{8,10},{9,11},{10,... | collective-permute-start | bytes 995336 | tf_op jit(solution)/shard_map/ppermute | solution.py:404
  44.9 8.6 %collective-permute-start = (bf16[144,1152]{1,0:T(8,128)(2,1)S(1)}, bf16[144,1152]{1,0:T(8,128)(2,1)S(1)}, u32[]{:S(2)}, u32[]{:S(2)}) collective-permute-start(bf16[144,1152]{1,0:T(8,128)(2,1)S(1)} %copy-done.10), channel_id=1, source_target_pairs={{0,1},{1,0},{2,3},{3,2},{4,5},{5,4},{6,7},{7,6},{8,9},{9,8},{10,11... | collective-permute-start | bytes 995336 | tf_op jit(solution)/shard_map/ppermute | solution.py:404
  44.9 8.6 %copy-start.11 = (bf16[144,1152]{1,0:T(8,128)(2,1)}, bf16[144,1152]{1,0:T(8,128)(2,1)S(1)}, u32[]{:S(2)}) copy-start(bf16[144,1152]{1,0:T(8,128)(2,1)S(1)} %collective-permute-done.1.refs_2_) | copy-start | bytes 995332
  44.9 8.6 %collective-permute-start.2 = (bf16[144,1152]{1,0:T(8,128)(2,1)S(1)}, bf16[144,1152]{1,0:T(8,128)(2,1)S(1)}, u32[]{:S(2)}, u32[]{:S(2)}) collective-permute-start(bf16[144,1152]{1,0:T(8,128)(2,1)S(1)} %collective-permute-done.1.refs_2_), channel_id=1, source_target_pairs={{0,1},{1,0},{2,3},{3,2},{4,5},{5,4},{6,7},{7,6},{8,9},{9,8},{10,11... | collective-permute-start | bytes 995336 | tf_op jit(solution)/shard_map/ppermute | solution.py:404
  45.4 14.2 %collective-permute-start.3 = (bf16[144,1152]{1,0:T(8,128)(2,1)}, bf16[144,1152]{1,0:T(8,128)(2,1)S(1)}, u32[]{:S(2)}, u32[]{:S(2)}) collective-permute-start(bf16[144,1152]{1,0:T(8,128)(2,1)} %get-tuple-element.37.refs_0_), channel_id=1, source_target_pairs={{0,1},{1,0},{2,3},{3,2},{4,5},{5,4},{6,7},{7,6},{8,9},{9,8},{10,11... | collective-permute-start | bytes 995336 | tf_op jit(solution)/shard_map/ppermute | solution.py:404
  50.7 9.0 %copy-start.4 = (bf16[144,1152]{1,0:T(8,128)(2,1)}, bf16[144,1152]{1,0:T(8,128)(2,1)S(1)}, u32[]{:S(2)}) copy-start(bf16[144,1152]{1,0:T(8,128)(2,1)S(1)} %collective-permute-done.4.refs_2_) | copy-start | bytes 995332
  50.7 9.0 %collective-permute-start.5 = (bf16[144,1152]{1,0:T(8,128)(2,1)S(1)}, bf16[144,1152]{1,0:T(8,128)(2,1)S(1)}, u32[]{:S(2)}, u32[]{:S(2)}) collective-permute-start(bf16[144,1152]{1,0:T(8,128)(2,1)S(1)} %collective-permute-done.4.refs_2_), channel_id=1, source_target_pairs={{0,1},{1,0},{2,3},{3,2},{4,5},{5,4},{6,7},{7,6},{8,9},{9,8},{10,11... | collective-permute-start | bytes 995336 | tf_op jit(solution)/shard_map/ppermute | solution.py:404
  53.5 0.7 copy-start.12
  53.5 0.8 copy-start.13
  59.7 0.7 copy-start.5
  59.7 0.8 copy-start.6
  102.7 7.3 %collective-permute-start.7 = (bf16[144,1152]{1,0:T(8,128)(2,1)}, bf16[144,1152]{1,0:T(8,128)(2,1)S(1)}, u32[]{:S(2)}, u32[]{:S(2)}) collective-permute-start(bf16[144,1152]{1,0:T(8,128)(2,1)} %get-tuple-element.41.refs_0_), channel_id=1, source_target_pairs={{0,2},{1,3},{2,0},{3,1},{4,6},{5,7},{6,4},{7,5},{8,10},{9,11},{10,... | collective-permute-start | bytes 995336 | tf_op jit(solution)/shard_map/ppermute | solution.py:404
  104.2 8.2 %collective-permute-start.6 = (bf16[144,1152]{1,0:T(8,128)(2,1)}, bf16[144,1152]{1,0:T(8,128)(2,1)S(1)}, u32[]{:S(2)}, u32[]{:S(2)}) collective-permute-start(bf16[144,1152]{1,0:T(8,128)(2,1)} %get-tuple-element.41.refs_0_), channel_id=1, source_target_pairs={{0,1},{1,0},{2,3},{3,2},{4,5},{5,4},{6,7},{7,6},{8,9},{9,8},{10,11... | collective-permute-start | bytes 995336 | tf_op jit(solution)/shard_map/ppermute | solution.py:404
  110.0 2.4 %copy-start.7 = (bf16[144,1152]{1,0:T(8,128)(2,1)}, bf16[144,1152]{1,0:T(8,128)(2,1)S(1)}, u32[]{:S(2)}) copy-start(bf16[144,1152]{1,0:T(8,128)(2,1)S(1)} %collective-permute-done.7.refs_2_) | copy-start | bytes 995332
  110.0 2.4 %collective-permute-start.8 = (bf16[144,1152]{1,0:T(8,128)(2,1)S(1)}, bf16[144,1152]{1,0:T(8,128)(2,1)S(1)}, u32[]{:S(2)}, u32[]{:S(2)}) collective-permute-start(bf16[144,1152]{1,0:T(8,128)(2,1)S(1)} %collective-permute-done.7.refs_2_), channel_id=1, source_target_pairs={{0,1},{1,0},{2,3},{3,2},{4,5},{5,4},{6,7},{7,6},{8,9},{9,8},{10,11... | collective-permute-start | bytes 995336 | tf_op jit(solution)/shard_map/ppermute | solution.py:404
  112.4 0.7 copy-start.8
  112.4 0.8 copy-start.9
  132.2 11.1 %all-to-all-start.5 = ((s16[8,96,128]{2,1,0:T(8,128)(2,1)}), s16[8,96,128]{2,1,0:T(8,128)(2,1)S(1)}, u32[]{:S(2)}, u32[]{:S(2)}) async-start(s16[8,96,128]{2,1,0:T(8,128)(2,1)} %mix_back.1), calls=%async_computation.5 | async-start | bytes 393216 | tf_op jit(solution)/shard_map/all_to_all | solution.py:410
  143.3 0.7 copy-start.3

commit v2 on v1

v2 whole, which is shorter than its diff:
```python
import functools

import jax
import jax.numpy as jnp
from jax import lax
from jax.experimental import pallas as pl
from jax.experimental.pallas import tpu as pltpu
from jax.sharding import PartitionSpec as P

exact_mode = lax.Precision.HIGHEST
f32 = jnp.float32
bf16 = jnp.bfloat16
i16 = jnp.int16
LEVELS = 32760.0
STEP = 0.08664339756999316
TINY = 1e-30
HALF = 64
UNROLLED = 16
GRANT = 12 << 20


def vmem():
    return pl.BlockSpec(memory_space=pltpu.VMEM)


def smem():
    return pl.BlockSpec(memory_space=pltpu.SMEM)


class Plan:
    def __init__(self, rows, width, chan, blk):
        assert rows % 16 == 0 and width % 128 in (0, HALF) and width >= 128
        self.rows, self.width, self.chan, self.blk = rows, width, chan, blk
        self.full = width // 128
        self.tail = width % 128 != 0
        self.groups = rows // 8
        self.main = self.full * 128
        self.wide = self.main + (128 if self.tail else 0)
        self.packed = 2 * self.main + (128 if self.tail else 0)
        self.tiles = self.groups * self.full + (self.groups // 2 if self.tail else 0)
        self.slots, rest = divmod(self.tiles, chan)
        self.extra = 0
        if rest and chan <= UNROLLED and 8 * rest % chan == 0 and 8 * rest // chan <= 4 and self.slots:
            self.extra = 8 * rest // chan
        elif rest:
            self.slots += 1
        self.pair_rows = 16 * (self.slots + 1)
        self.single_rows = 8 * (self.slots + 1)

    def load(self, ref, u):
        if u >= self.tiles:
            return jnp.zeros((8, 128), f32)
        if u < self.groups * self.full:
            g, j = divmod(u, self.full)
            return ref[8 * g : 8 * g + 8, 128 * j : 128 * j + 128]
        v = 16 * (u - self.groups * self.full)
        first = ref[v : v + 8, self.main : self.wide]
        second = pltpu.roll(ref[v + 8 : v + 16, self.main : self.wide], HALF, 1)
        return jnp.where(low_lanes((8, 128)), first, second)

    def store(self, ref, u, tile):
        if u >= self.tiles:
            return
        if u < self.groups * self.full:
            g, j = divmod(u, self.full)
            ref[8 * g : 8 * g + 8, 128 * j : 128 * j + 128] = tile
            return
        v = 16 * (u - self.groups * self.full)
        ref[v : v + 8, self.main : self.wide] = tile
        ref[v + 8 : v + 16, self.main : self.wide] = pltpu.roll(tile, HALF, 1)


def low_lanes(shape):
    return lax.broadcasted_iota(jnp.int32, shape, len(shape) - 1) < HALF


def sublane():
    return lax.broadcasted_iota(jnp.int32, (8, 128), 0)


def turn(tile, by):
    by %= 8
    return pltpu.roll(tile, by, 0) if by else tile


def lower(tile):
    return jnp.where(sublane() < 4, tile, turn(tile, 4))


def spread(tile):
    other = turn(tile, 4)
    low = sublane() < 4
    return jnp.concatenate([jnp.where(low, tile, other), jnp.where(low, other, tile)], axis=0)


def exponent_of(peak):
    return jnp.floor(jnp.log(jnp.maximum(peak, TINY)) * (1.0 / STEP)) + 1.0


def scale_up(e):
    return jnp.exp(e * -STEP) * LEVELS


def scale_down(e):
    return jnp.exp(e * STEP) * (1.0 / LEVELS)


def to_int(value):
    return jnp.round(value).astype(jnp.int32).astype(i16)


def from_int(value):
    return value.astype(jnp.int32).astype(f32)


def largest(values):
    return functools.reduce(jnp.maximum, [jnp.abs(v) for v in values])


def take_extra(plan, ref, chunk, at):
    out = jnp.zeros((8, 128), f32)
    for m in range(plan.extra):
        tile, row = divmod(chunk * plan.extra + m, 8)
        value = plan.load(ref, plan.chan * plan.slots + tile)
        out = jnp.where(sublane() == at + m, turn(value, at + m - row), out)
    return out


def put_extra(plan, ref, extras, at):
    if not plan.extra:
        return
    tiles = [jnp.zeros((8, 128), f32) for _ in range(plan.chan * plan.extra // 8)]
    for chunk, value in enumerate(extras):
        for m in range(plan.extra):
            tile, row = divmod(chunk * plan.extra + m, 8)
            tiles[tile] = jnp.where(sublane() == row, turn(value, row - at - m), tiles[tile])
    for tile, value in enumerate(tiles):
        plan.store(ref, plan.chan * plan.slots + tile, value)


def encode_pair(plan, values, extra, write):
    peak = largest(values)
    first = jnp.maximum(peak[0:8], turn(peak[0:8], 4))
    second = jnp.maximum(peak[8:16], turn(peak[8:16], 4))
    peak = jnp.maximum(jnp.where(sublane() < 4, first, second), jnp.abs(extra))
    e = exponent_of(peak)
    up = scale_up(e)
    both = spread(up)
    for p, v in enumerate(values):
        write(p, to_int(v * both))
    write(plan.slots, to_int(jnp.concatenate([e, extra * up], axis=0)))


def pair_scale(plan, in_ref, chunk):
    last = from_int(in_ref[chunk, 16 * plan.slots : 16 * plan.slots + 16, :])
    down = scale_down(last[0:8])
    return spread(down), last[8:16] * down


def write_pair(out_ref, chunk):
    def write(p, tile):
        out_ref[chunk, 16 * p : 16 * p + 16, :] = tile

    return write


def pack_pair(plan, first_ref, second_ref, out_ref):
    for chunk in range(plan.chan):
        us = [chunk * plan.slots + p for p in range(plan.slots)]
        values = [jnp.concatenate([plan.load(first_ref, u), plan.load(second_ref, u)], axis=0) for u in us]
        extra = take_extra(plan, first_ref, chunk, 0) + take_extra(plan, second_ref, chunk, 4)
        encode_pair(plan, values, extra, write_pair(out_ref, chunk))


def unpack_pair(plan, in_ref, first_ref, second_ref):
    extras = []
    for chunk in range(plan.chan):
        down, extra = pair_scale(plan, in_ref, chunk)
        extras.append(extra)
        for p in range(plan.slots):
            u = chunk * plan.slots + p
            if u < plan.tiles:
                v = from_int(in_ref[chunk, 16 * p : 16 * p + 16, :]) * down
                plan.store(first_ref, u, v[0:8])
                plan.store(second_ref, u, v[8:16])
    put_extra(plan, first_ref, extras, 0)
    put_extra(plan, second_ref, extras, 4)


def encode_single(plan, values, extra, out_ref, chunk):
    peak = jnp.maximum(largest(values), jnp.abs(extra))
    e = exponent_of(jnp.maximum(peak, turn(peak, 4)))
    up = scale_up(e)
    scaled = [v * up for v in values] + [jnp.where(sublane() < 4, e, extra * up)]
    for p in range(0, len(scaled), 2):
        part = scaled[p : p + 2]
        out_ref[chunk, 8 * p : 8 * (p + len(part)), :] = to_int(jnp.concatenate(part, axis=0))


def decode_single(plan, in_ref, chunk):
    rows = from_int(in_ref[chunk, 8 * plan.slots : 8 * plan.slots + 8, :])
    down = scale_down(lower(rows))
    values = []
    for p in range(plan.slots):
        values.append(from_int(in_ref[chunk, 8 * p : 8 * p + 8, :]) * down)
    return values, rows * down


def pack_single(plan, ref, out_ref):
    for chunk in range(plan.chan):
        values = [plan.load(ref, chunk * plan.slots + p) for p in range(plan.slots)]
        encode_single(plan, values, take_extra(plan, ref, chunk, 4), out_ref, chunk)


def unpack_single(plan, in_ref, ref):
    extras = []
    for chunk in range(plan.chan):
        values, extra = decode_single(plan, in_ref, chunk)
        extras.append(extra)
        for p, value in enumerate(values):
            plan.store(ref, chunk * plan.slots + p, value)
    put_extra(plan, ref, extras, 4)


def store_packed(plan, first, second, out_ref):
    m = plan.main
    out_ref[:, 0:m] = first[:, 0:m].astype(bf16)
    out_ref[:, m : 2 * m] = second[:, 0:m].astype(bf16)
    if plan.tail:
        a = first[:, m : plan.wide]
        b = pltpu.roll(second[:, m : plan.wide], HALF, 1)
        out_ref[:, 2 * m :] = jnp.where(low_lanes(a.shape), a, b).astype(bf16)


def assemble(plan, pieces, blk_ref, out_ref):
    for s, piece in enumerate(pieces):
        at = pl.multiple_of((blk_ref[0] ^ s) * plan.rows, 16)
        out_ref[pl.ds(at, plan.rows), :] = piece[...]


def dot(a, b):
    return jnp.dot(a, b, preferred_element_type=f32)


def product(plan, left, right_ref, second, main_ref, tail):
    m = plan.main
    at = m if second else 0
    main = dot(left, right_ref[:, at : at + m])
    if not plan.tail:
        return main, None
    last = dot(left, right_ref[:, 2 * m :])
    return main, (pltpu.roll(last, HALF, 1) if second else last)


def commute(plan, left, right_ref, right_second, other_left, other_ref, other_second, out_ref):
    a, a_tail = product(plan, left, right_ref, right_second, None, None)
    b, b_tail = product(plan, other_left, other_ref, other_second, None, None)
    out_ref[:, 0 : plan.main] = a - b
    if plan.tail:
        out_ref[:, plan.main : plan.wide] = a_tail - b_tail


def inside_of(plan, size, blk):
    shape = (plan.rows, plan.width)
    row = lax.broadcasted_iota(jnp.int32, shape, 0) + blk[0] * plan.rows
    col = lax.broadcasted_iota(jnp.int32, shape, 1)
    return (row < size[0]) & (col < size[0])


def kernel_enter(plan, omega, ham, occ, size, blk, send, packed, left_gen, left_ham, gen_s, ham_s):
    inside = inside_of(plan, size, blk)
    gen = jnp.where(inside, omega[...], 0.0)
    start = jnp.where(inside, ham[...], 0.0)
    gen_s[:, 0 : plan.width] = gen
    ham_s[:, 0 : plan.width] = start
    left_gen[...] = (gen * occ[...]).astype(bf16)
    left_ham[...] = (start * occ[...]).astype(bf16)
    pack_pair(plan, gen_s, ham_s, send)
    store_packed(plan, gen_s, ham_s, packed)


def kernel_prepare(plan, column_map, occ, select, moved_occ):
    w = plan.width
    rows = lax.broadcasted_iota(jnp.int32, (w, w), 0)
    hot = (rows == column_map[...]).astype(f32).astype(bf16)
    select[...] = hot
    value = occ[...]
    high = value.astype(bf16)
    rest = value - high.astype(f32)
    middle = rest.astype(bf16)
    low = (rest - middle.astype(f32)).astype(bf16)
    total = jnp.zeros((8, w), f32)
    for part in (low, middle, high):
        total = total + lax.dot_general(
            jnp.broadcast_to(part.astype(f32), (8, w)).astype(bf16),
            hot,
            (((1,), (1,)), ((), ())),
            preferred_element_type=f32,
        )
    moved_occ[...] = total[0:1]


def kernel_unpack_cross(plan, recv, moved_occ, packed, scaled_gen, scaled_ham, gen, ham):
    unpack_pair(plan, recv, gen, ham)
    store_packed(plan, gen, ham, packed)
    scaled_gen[...] = (gen[:, 0 : plan.width] * moved_occ[...]).astype(bf16)
    scaled_ham[...] = (ham[:, 0 : plan.width] * moved_occ[...]).astype(bf16)


def keep_first(plan, right, kept):
    m = plan.main
    kept[:, 0:m] = right[:, 0:m]
    if plan.tail:
        kept[:, m:] = right[:, 2 * m :]


def kernel_cross_left(plan, scaled_gen, scaled_ham, select, cross_gen, cross_ham):
    cross_gen[...] = dot(scaled_gen[...], select[...]).astype(bf16)
    cross_ham[...] = dot(scaled_ham[...], select[...]).astype(bf16)


def kernel_first_pair(plan, left_gen, left_ham, blk, *refs):
    pieces, (right_gen, first, right) = refs[: plan.blk], refs[plan.blk :]
    assemble(plan, pieces, blk, right)
    commute(plan, left_gen[...], right, True, left_ham[...], right, False, first)
    keep_first(plan, right, right_gen)


def kernel_first_cross(plan, left_gen, left_ham, first, blk, *refs):
    pieces, (right_gen, send, right, cross_s) = refs[: plan.blk], refs[plan.blk :]
    assemble(plan, pieces, blk, right)
    commute(plan, left_gen[...], right, True, left_ham[...], right, False, cross_s)
    keep_first(plan, right, right_gen)
    pack_pair(plan, cross_s, first, send)


def kernel_unpack_eta(plan, recv, first, occ, moved_occ, cross_rows, eta_rows, eta, left_eta, scaled_cross, cross):
    w = plan.width
    unpack_pair(plan, recv, eta, cross)
    eta[...] = eta[...] + first[...]
    cross_rows[...] = cross[:, 0:w].astype(bf16)
    eta_rows[...] = eta[:, 0:w].astype(bf16)
    left_eta[...] = (eta[:, 0:w] * occ[...]).astype(bf16)
    scaled_cross[...] = (cross[:, 0:w] * moved_occ[...]).astype(bf16)


def kernel_eta_left(plan, scaled_cross, select, left_cross):
    left_cross[...] = dot(scaled_cross[...], select[...]).astype(bf16)


def kernel_second_cross(plan, left_gen, left_eta, right_gen, blk, *refs):
    pieces, (send, right, cross_s) = refs[: plan.blk], refs[plan.blk :]
    w = plan.width
    assemble(plan, pieces, blk, right)
    cross_s[:, 0:w] = dot(left_gen[...], right[...]) - dot(left_eta[...], right_gen[:, 0:w])
    pack_single(plan, cross_s, send)


def kernel_second_pair(plan, left_gen, left_eta, right_gen, blk, *refs):
    pieces, (second, right) = refs[: plan.blk], refs[plan.blk :]
    assemble(plan, pieces, blk, right)
    second[...] = dot(left_gen[...], right[...]) - dot(left_eta[...], right_gen[:, 0 : plan.width])


def kernel_finish(plan, recv, ham, eta, second, size, blk, out, back_s):
    unpack_single(plan, recv, back_s)
    w = plan.width
    total = ham[...] + eta[:, 0:w] + 0.5 * (second[...] + back_s[:, 0:w])
    out[...] = jnp.where(inside_of(plan, size, blk), total, 0.0)


def mixed(mixing, values, transposed):
    n = len(values)
    out = []
    for k in range(n):
        terms = [values[c] * (mixing[c, k] if transposed else mixing[k, c]) for c in range(n)]
        out.append(functools.reduce(jnp.add, terms))
    return out


def both_of(mixing, first, second):
    restored = mixed(mixing, first, True)
    crossed = mixed(mixing, [v + r for v, r in zip(second, restored)], False)
    return restored, crossed


def kernel_mix_pair(plan, both, mixing, recv, send, kept):
    n = plan.chan
    scales = [pair_scale(plan, recv, c) for c in range(n)]
    extra = [s[1] for s in scales]
    if both:
        restored, crossed = both_of(mixing, extra, [turn(x, 4) for x in extra])
        extra = [jnp.where(sublane() < 4, r, turn(x, 4)) for r, x in zip(restored, crossed)]
    else:
        extra = mixed(mixing, extra, False)
    for p in range(plan.slots):
        values = [from_int(recv[c, 16 * p : 16 * p + 16, :]) * scales[c][0] for c in range(n)]
        if both:
            pairs = zip(*both_of(mixing, [v[0:8] for v in values], [v[8:16] for v in values]))
            result = [jnp.concatenate(pair, axis=0) for pair in pairs]
        else:
            result = mixed(mixing, values, False)
        for k in range(n):
            kept[k, 16 * p : 16 * p + 16, :] = result[k]
    for k in range(n):
        values = [kept[k, 16 * p : 16 * p + 16, :] for p in range(plan.slots)]
        encode_pair(plan, values, extra[k], write_pair(send, k))


def kernel_mix_single(plan, both, mixing, recv, send, kept):
    n = plan.chan
    downs, extra = [], []
    for c in range(n):
        rows = from_int(recv[c, 8 * plan.slots : 8 * plan.slots + 8, :])
        downs.append(scale_down(lower(rows)))
        extra.append(rows * downs[c])
    extra = mixed(mixing, extra, True)
    for p in range(plan.slots):
        result = mixed(mixing, [from_int(recv[c, 8 * p : 8 * p + 8, :]) * downs[c] for c in range(n)], True)
        for k in range(n):
            kept[k, 8 * p : 8 * p + 8, :] = result[k]
    for k in range(n):
        values = [kept[k, 8 * p : 8 * p + 8, :] for p in range(plan.slots)]
        encode_single(plan, values, extra[k], send, k)


def plain_mix(plan, kind, mixing, recv):
    n, slots = plan.chan, plan.slots

    def mix(spec, value):
        return jnp.einsum(spec, mixing, value, precision=exact_mode, preferred_element_type=f32)

    def spread_rows(e):
        if kind == "back":
            return jnp.concatenate([e[:, 0:4]] * 2, axis=1)
        return jnp.concatenate([e[:, 0:4]] * 2 + [e[:, 4:8]] * 2, axis=1)

    raw = recv.astype(jnp.int32).astype(f32)
    high = 8 if kind == "back" else 16
    e = raw[:, high * slots : high * slots + 8]
    body = raw[:, 0 : high * slots].reshape(n, slots, high, 128) * scale_down(spread_rows(e))[:, None]
    if kind == "cross":
        result = mix("kc,cpsl->kpsl", body)
    elif kind == "both":
        restored = mix("ck,cpsl->kpsl", body[:, :, 0:8])
        crossed = mix("kc,cpsl->kpsl", body[:, :, 8:16] + restored)
        result = jnp.concatenate([restored, crossed], axis=2)
    else:
        result = mix("ck,cpsl->kpsl", body)
    peak = jnp.max(jnp.abs(result), axis=1)
    peak = jnp.max(peak.reshape(n, high // 8, 2, 4, 128), axis=2).reshape(n, high // 2, 128)
    e = exponent_of(peak)
    scaled = result * scale_up(spread_rows(e))[:, None]
    out = jnp.concatenate([scaled.reshape(n, -1, 128), e], axis=1)
    out = jnp.pad(out, ((0, 0), (0, recv.shape[1] - out.shape[1]), (0, 0)))
    return to_int(out)


def near(value):
    return pltpu.with_memory_space_constraint(value, pltpu.VMEM)


def call(body, plan, outs, specs, scratch=(), flops=0, final=False):
    def run(*operands):
        places = {"v": pltpu.VMEM, "h": pltpu.HBM}
        placed = [
            pltpu.with_memory_space_constraint(x, places[s]) if s in places else x
            for x, s in zip(operands, specs, strict=True)
        ]
        return pl.pallas_call(
            functools.partial(body, plan),
            out_shape=tuple((jax.ShapeDtypeStruct if final else pltpu.VMEM)(s, d) for s, d in outs),
            in_specs=[smem() if s == "s" else vmem() for s in specs],
            out_specs=tuple(vmem() for _ in outs),
            scratch_shapes=tuple(pltpu.VMEM(s, d) for s, d in scratch),
            name=body.__name__,
            cost_estimate=pl.CostEstimate(flops=flops or plan.rows * plan.width * 60000, transcendentals=0, bytes_accessed=0),
            compiler_params=pltpu.CompilerParams(vmem_limit_bytes=GRANT),
        )(*placed)

    return run


def mix_call(plan, kind, mixing, recv):
    if plan.chan > UNROLLED:
        return plain_mix(plan, kind, mixing, recv)
    body = kernel_mix_single if kind == "back" else kernel_mix_pair
    return pl.pallas_call(
        functools.partial(body, plan, kind == "both"),
        out_shape=pltpu.VMEM(recv.shape, i16),
        in_specs=[smem(), vmem()],
        out_specs=vmem(),
        scratch_shapes=(pltpu.VMEM((plan.chan, recv.shape[1], 128), f32),),
        name="mix_" + kind,
        compiler_params=pltpu.CompilerParams(vmem_limit_bytes=GRANT),
    )(mixing, near(recv))


def mixing_matrix(jlabel, family, sixj):
    levels = sixj.shape[0]
    one_hot = (jlabel[:, None] == jnp.arange(levels, dtype=jnp.int32)[None, :]).astype(f32)
    picked = jnp.dot(one_hot, sixj, precision=exact_mode, preferred_element_type=f32)
    picked = jnp.dot(picked, one_hot.T, precision=exact_mode, preferred_element_type=f32)
    kindred = (family[:, None] == family[None, :]).astype(f32)
    return picked * kindred


def swap(value, size, bits):
    return lax.ppermute(value, "blk", [(b, b ^ bits) for b in range(size)])


def far_rows(value, size):
    return swap(value, size, size // 2) if size > 1 else None


def near_rows(value, far, size):
    pieces = {0: value}
    bit = size // 2
    while bit:
        for s, piece in list(pieces.items()):
            pieces[s ^ bit] = far if bit == size // 2 and s == 0 else swap(piece, size, bit)
        bit //= 2
    return [pieces[s] for s in range(size)]


def exchange(value):
    return lax.all_to_all(value, "chan", 0, 0, tiled=True)


def on_device(omega, hamiltonian, pair_occ, cross_occ, block_size, jlabel, family, sixj, column_map):
    channels_here, rows, width = omega.shape
    assert channels_here == 1
    chan, blk = lax.axis_size("chan"), lax.axis_size("blk")
    assert blk & (blk - 1) == 0
    plan = Plan(rows, width, chan, blk)
    omega, ham = omega[0], hamiltonian[0]
    blk_index = lax.axis_index("blk").astype(jnp.int32).reshape(1)
    pair = ((chan, plan.pair_rows, 128), i16)
    single = ((chan, plan.single_rows, 128), i16)
    packed = ((rows, plan.packed), bf16)
    left = ((rows, width), bf16)
    plain = ((rows, width), f32)
    wide = ((rows, plan.wide), f32)
    right = ((rows * blk, plan.packed), bf16)
    right_kept = ((rows * blk, plan.wide), bf16)
    right_one = ((rows * blk, width), bf16)

    send, pair_rows, left_gen, left_ham = call(
        kernel_enter, plan, [pair, packed, left, left], "hhhss", [wide, wide]
    )(omega, ham, pair_occ, block_size, blk_index)
    select, moved_occ = call(kernel_prepare, plan, [((width, width), bf16), ((1, width), f32)], "vv")(
        column_map.reshape(1, width), cross_occ
    )
    mixing = mixing_matrix(jlabel, family, sixj)
    pair_far = far_rows(pair_rows, blk)
    recv = exchange(send)
    recv, mixing, select, moved_occ, pair_far = lax.optimization_barrier((recv, mixing, select, moved_occ, pair_far))
    pair_pieces = near_rows(pair_rows, pair_far, blk)
    recv = exchange(mix_call(plan, "cross", mixing, recv))
    pair_right, first = call(kernel_first_pair, plan, [right_kept, wide], "vvs" + "v" * blk, [right])(
        left_gen, left_ham, blk_index, *pair_pieces
    )
    recv, pair_right, first = lax.optimization_barrier((recv, pair_right, first))
    cross_rows, scaled_gen, scaled_ham = call(
        kernel_unpack_cross, plan, [packed, left, left], "vv", [wide, wide]
    )(recv, moved_occ)
    cross_pieces = near_rows(cross_rows, far_rows(cross_rows, blk), blk)
    cross_gen_left, cross_ham_left = call(kernel_cross_left, plan, [left, left], "vvv")(scaled_gen, scaled_ham, select)
    cross_right, send = call(
        kernel_first_cross, plan, [right_kept, pair], "vvvs" + "v" * blk, [right, wide]
    )(cross_gen_left, cross_ham_left, first, blk_index, *cross_pieces)
    recv = exchange(mix_call(plan, "both", mixing, exchange(send)))
    cross_rows, eta_rows, eta, left_eta, scaled_cross = call(
        kernel_unpack_eta, plan, [left, left, wide, left, left], "vvvv", [wide]
    )(recv, first, pair_occ, moved_occ)
    cross_far = far_rows(cross_rows, blk)
    eta_far = far_rows(eta_rows, blk)
    cross_pieces = near_rows(cross_rows, cross_far, blk)
    (cross_eta_left,) = call(kernel_eta_left, plan, [left], "vv")(scaled_cross, select)
    (send,) = call(kernel_second_cross, plan, [single], "vvvs" + "v" * blk, [right_one, wide])(
        cross_gen_left, cross_eta_left, cross_right, blk_index, *cross_pieces
    )
    send, eta_far = lax.optimization_barrier((send, eta_far))
    recv = exchange(send)
    eta_pieces = near_rows(eta_rows, eta_far, blk)
    (second,) = call(kernel_second_pair, plan, [plain], "vvvs" + "v" * blk, [right_one])(
        left_gen, left_eta, pair_right, blk_index, *eta_pieces
    )
    recv, second = lax.optimization_barrier((recv, second))
    recv = exchange(mix_call(plan, "back", mixing, recv))
    (out,) = call(kernel_finish, plan, [plain], "vhvvss", [wide], final=True)(
        recv, ham, eta, second, block_size, blk_index
    )
    return out[None]


def solution(mesh):
    in_specs = (
        P("chan", "blk", None),
        P("chan", "blk", None),
        P("chan", None),
        P("chan", None),
        P("chan"),
        P(),
        P(),
        P(),
        P(),
    )
    out_specs = P("chan", "blk", None)
    return jax.shard_map(
        on_device, mesh=mesh, in_specs=in_specs, out_specs=out_specs, check_vma=False
    )
```

time: 147 us -> 123 us (0.84)
  Pallas kernels: 35.1 us -> 13.7 us
  blocking collectives: 48.1 us -> 40.9 us
  waiting for transfers between devices: 36.3 us -> 41.7 us
    pallas_call x14, Pallas kernels: 35.1 us -> 13.7 us  [the longest x11 9.54 us: run(): pl.pallas_call(functools.partial(body, plan), out_shape=tuple(((jax.Shape...]
    all_to_all x3, blocking collectives: 48.1 us -> 40.9 us  [exchange(): return lax.all_to_all(value, 'chan', 0, 0, tiled=True)]
    ppermute x9 -> x12, waiting for transfers between devices: 11 us -> 15.8 us  [swap(): return lax.ppermute(value, 'blk', [(b, b ^ bits) for b in range(size)])]
    all_to_all x3, starting transfers between devices: 14.5 us -> 13 us  [exchange(): return lax.all_to_all(value, 'chan', 0, 0, tiled=True)]
    ppermute x9 -> x12, starting transfers between devices: 5.21 us -> 6.26 us  [swap(): return lax.ppermute(value, 'blk', [(b, b ^ bits) for b in range(size)])]
    unnamed x34 -> x30, local copies, waits for them, and re-layouts: 4.66 us -> 5.1 us
  transfers between devices with their start and end apart: 12 -> 15, of which waited for: 5 -> 8; matrix products, arithmetic and copies ran while one was open for 1% -> 0% of each run, Pallas kernels for 10% -> 5%
where the time goes in v2:
time: 123 us; the launch traced here: 122 us
  waiting for transfers between devices  41.7 us (34%)
  blocking collectives  40.9 us (33%)
  starting transfers between devices  19.2 us (16%)
  Pallas kernels  13.7 us (11%)
  local copies, waits for them, and re-layouts  5.1 us (4%)
    all_to_all x3, blocking collectives, exchange(): return lax.all_to_all(value, 'chan', 0, 0, tiled=True)  40.9 us
    all_to_all x3, waiting for transfers between devices, exchange(): return lax.all_to_all(value, 'chan', 0, 0, tiled=True)  25.8 us
    ppermute x12, waiting for transfers between devices, swap(): return lax.ppermute(value, 'blk', [(b, b ^ bits) for b in range(size)])  15.8 us
    all_to_all x3, starting transfers between devices, exchange(): return lax.all_to_all(value, 'chan', 0, 0, tiled=True)  13 us
    pallas_call x11, Pallas kernels, run(): pl.pallas_call(functools.partial(body, plan), out_shape=tuple(((jax.Shape...  9.54 us
    ppermute x12, starting transfers between devices, swap(): return lax.ppermute(value, 'blk', [(b, b ^ bits) for b in range(size)])  6.26 us
    unnamed x30, local copies, waits for them, and re-layouts  5.1 us
    pallas_call x3, Pallas kernels, mix_call(): pl.pallas_call(functools.partial(body, plan, kind == 'both'), out_shape=p...  4.12 us
  transfers between devices with their start and end apart: 15, of which 8 were waited for; matrix products, arithmetic and copies ran while one was open for 0% of the time, Pallas kernels for 5%

profile of v2, /device:TPU:0, one launch (start us, length us, event | category | flops | bytes accessed | tf_op | source)
XLA Modules:
  0.0 121.8 jit_solution(7891703188001964983)
XLA Ops:
  0.7 2.1 %kernel_enter.1 = (s16[8,176,128]{2,1,0:T(8,128)(2,1)}, bf16[144,1152]{1,0:T(8,128)(2,1)S(1)}, bf16[144,576]{1,0:T(8,128)(2,1)S(1)}, bf16[144,576]{1,0:T(8,128)(2,1)S(1)}) custom-call(f32[144,576]{1,0:T(8,128)} %bitcast.6, f32[144,576]{1,0:T(8,128)} %bitcast.7, f32[1,576]{1,0:T(1,128)} %occ.5, s32[1]{0:T(128)S(6)} %copy.10.size, s32[1]{0:T(128)} %bitcast.2.blk), custom_call_target="tpu_custom_call" | custom-call | flops 4976640000 | tf_op jit(solution)/shard_map/kernel_enter/pallas_call | solution.py:470
  2.8 0.7 copy-done.5
  3.4 0.7 copy-done.10
  4.1 0.5 collective-permute-start.1
  4.6 2.5 %collective-permute-start = (bf16[144,1152]{1,0:T(8,128)(2,1)S(1)}, bf16[144,1152]{1,0:T(8,128)(2,1)S(1)}, u32[]{:S(2)}, u32[]{:S(2)}) collective-permute-start(bf16[144,1152]{1,0:T(8,128)(2,1)S(1)} %get-tuple-element.40.refs_0_), channel_id=1, source_target_pairs={{0,2},{1,3},{2,0},{3,1},{4,6},{5,7},{6,4},{7,5},{8,10},{9,11},{10,... | collective-permute-start | bytes 995336 | tf_op jit(solution)/shard_map/ppermute | solution.py:509
  7.1 5.9 %all-to-all-start = ((s16[8,176,128]{2,1,0:T(8,128)(2,1)}), s16[8,176,128]{2,1,0:T(8,128)(2,1)S(1)}, u32[]{:S(2)}, u32[]{:S(2)}) async-start(s16[8,176,128]{2,1,0:T(8,128)(2,1)} %get-tuple-element.37), calls=%async_computation | async-start | bytes 720896 | tf_op jit(solution)/shard_map/all_to_all | solution.py:527
  13.1 0.0 copy-start.1
  13.1 0.7 copy-done.1
  13.7 0.8 kernel_prepare.1
  14.6 0.0 copy-start.14
  14.6 0.2 fusion
  14.8 0.5 copy-done.14
  15.2 0.2 convolution_select_fusion.mixing
  15.4 0.2 collective-permute-done.refs_2_
  15.6 8.8 %all-to-all-done.recv = s16[8,176,128]{2,1,0:T(8,128)(2,1)S(1)} async-done(((s16[8,176,128]{2,1,0:T(8,128)(2,1)}), s16[8,176,128]{2,1,0:T(8,128)(2,1)S(1)}, u32[]{:S(2)}, u32[]{:S(2)}) %all-to-all-start) | async-done | bytes 360480 | tf_op jit(solution)/shard_map/all_to_all | solution.py:527
  24.4 1.9 %mix_cross.1 = s16[8,176,128]{2,1,0:T(8,128)(2,1)} custom-call(f32[8,8]{1,0:T(8,128)S(1)} %convolution_select_fusion.mixing, s16[8,176,128]{2,1,0:T(8,128)(2,1)S(1)} %all-to-all-done.recv), custom_call_target="tpu_custom_call" | custom-call | tf_op jit(solution)/shard_map/mix_cross/pallas_call | solution.py:488
  26.3 3.6 %all-to-all-start.1 = ((s16[8,176,128]{2,1,0:T(8,128)(2,1)}), s16[8,176,128]{2,1,0:T(8,128)(2,1)S(1)}, u32[]{:S(2)}, u32[]{:S(2)}) async-start(s16[8,176,128]{2,1,0:T(8,128)(2,1)} %mix_cross.1), calls=%async_computation.1 | async-start | bytes 720896 | tf_op jit(solution)/shard_map/all_to_all | solution.py:527
  30.0 0.9 copy-done.6
  30.9 0.9 copy-done.11
  31.9 0.6 kernel_first_pair.1
  32.5 9.2 %all-to-all-done.1.recv = s16[8,176,128]{2,1,0:T(8,128)(2,1)S(1)} async-done(((s16[8,176,128]{2,1,0:T(8,128)(2,1)}), s16[8,176,128]{2,1,0:T(8,128)(2,1)S(1)}, u32[]{:S(2)}, u32[]{:S(2)}) %all-to-all-start.1) | async-done | bytes 360480 | tf_op jit(solution)/shard_map/all_to_all | solution.py:527
  41.6 0.2 kernel_unpack_cross.1
  41.9 0.6 collective-permute-start.4
  42.4 8.6 %collective-permute-done.4.refs_2_ = bf16[144,1152]{1,0:T(8,128)(2,1)S(1)} collective-permute-done((bf16[144,1152]{1,0:T(8,128)(2,1)S(1)}, bf16[144,1152]{1,0:T(8,128)(2,1)S(1)}, u32[]{:S(2)}, u32[]{:S(2)}) %collective-permute-start.4) | collective-permute-done | bytes 331808 | tf_op jit(solution)/shard_map/ppermute | solution.py:509
  51.0 0.5 kernel_cross_left.1
  51.5 1.1 collective-permute-done.5.refs_3_
  52.6 0.8 kernel_first_cross.1
  53.5 15.9 %all_to_all.30.recv = s16[8,176,128]{2,1,0:T(8,128)(2,1)S(1)} all-to-all(s16[8,176,128]{2,1,0:T(8,128)(2,1)S(1)} %get-tuple-element.57), channel_id=1, replica_groups=mesh['chan'=8,'blk'=4] {'chan'}, dimensions={0} | all-to-all | bytes 720896 | tf_op jit(solution)/shard_map/all_to_all | solution.py:527
  69.4 1.2 %mix_both.1 = s16[8,176,128]{2,1,0:T(8,128)(2,1)S(1)} custom-call(f32[8,8]{1,0:T(8,128)S(1)} %convolution_select_fusion.mixing, s16[8,176,128]{2,1,0:T(8,128)(2,1)S(1)} %all_to_all.30.recv), custom_call_target="tpu_custom_call" | custom-call | tf_op jit(solution)/shard_map/mix_both/pallas_call | solution.py:488
  70.6 0.0 copy-start.2
  70.6 14.3 %all_to_all.31.recv = s16[8,176,128]{2,1,0:T(8,128)(2,1)S(1)} all-to-all(s16[8,176,128]{2,1,0:T(8,128)(2,1)S(1)} %mix_both.1), channel_id=1, replica_groups=mesh['chan'=8,'blk'=4] {'chan'}, dimensions={0} | all-to-all | bytes 720896 | tf_op jit(solution)/shard_map/all_to_all | solution.py:527
  84.9 0.3 kernel_unpack_eta.1
  85.2 0.7 copy-done.3
  85.9 0.5 collective-permute-start.7
  86.4 0.5 collective-permute-start.10
  86.9 1.5 %collective-permute-start.9 = (bf16[144,576]{1,0:T(8,128)(2,1)S(1)}, bf16[144,576]{1,0:T(8,128)(2,1)S(1)}, u32[]{:S(2)}, u32[]{:S(2)}) collective-permute-start(bf16[144,576]{1,0:T(8,128)(2,1)S(1)} %get-tuple-element.61.refs_0_), channel_id=1, source_target_pairs={{0,2},{1,3},{2,0},{3,1},{4,6},{5,7},{6,4},{7,5},{8,10},{9,11},{10,... | collective-permute-start | bytes 497672 | tf_op jit(solution)/shard_map/ppermute | solution.py:509
  88.5 4.9 %collective-permute-done.7.refs_2_ = bf16[144,576]{1,0:T(8,128)(2,1)S(1)} collective-permute-done((bf16[144,576]{1,0:T(8,128)(2,1)S(1)}, bf16[144,576]{1,0:T(8,128)(2,1)S(1)}, u32[]{:S(2)}, u32[]{:S(2)}) %collective-permute-start.7) | collective-permute-done | bytes 165920 | tf_op jit(solution)/shard_map/ppermute | solution.py:509
  93.4 0.3 kernel_eta_left.1.left_eta
  93.7 1.1 collective-permute-done.8.refs_3_
  94.8 1.4 %kernel_second_cross.1 = s16[8,88,128]{2,1,0:T(8,128)(2,1)} custom-call(bf16[144,576]{1,0:T(8,128)(2,1)S(1)} %get-tuple-element.53.left_gen, bf16[144,576]{1,0:T(8,128)(2,1)S(1)} %kernel_eta_left.1.left_eta, bf16[576,640]{1,0:T(8,128)(2,1)S(1)} %get-tuple-element.59.right_gen, s32[1]{0:T(128)} %bitcast.2.blk, ...), custom_call_target="tpu_custom_call" | custom-call | flops 4976640000 | tf_op jit(solution)/shard_map/kernel_second_cross/pallas_call | solution.py:470
  96.2 0.1 collective-permute-start.11
  96.4 3.4 %all-to-all-start.4 = ((s16[8,88,128]{2,1,0:T(8,128)(2,1)}), s16[8,88,128]{2,1,0:T(8,128)(2,1)S(1)}, u32[]{:S(2)}, u32[]{:S(2)}) async-start(s16[8,88,128]{2,1,0:T(8,128)(2,1)} %kernel_second_cross.1), calls=%async_computation.4 | async-start | bytes 360448 | tf_op jit(solution)/shard_map/all_to_all | solution.py:527
  99.8 0.6 kernel_second_pair.1.second
  100.4 0.0 copy-start.4
  100.4 7.8 %all-to-all-done.4.recv = s16[8,88,128]{2,1,0:T(8,128)(2,1)S(1)} async-done(((s16[8,88,128]{2,1,0:T(8,128)(2,1)}), s16[8,88,128]{2,1,0:T(8,128)(2,1)S(1)}, u32[]{:S(2)}, u32[]{:S(2)}) %all-to-all-start.4) | async-done | bytes 180256 | tf_op jit(solution)/shard_map/all_to_all | solution.py:527
  108.2 1.0 mix_back.1
  109.2 10.7 %all_to_all.32.recv = s16[8,88,128]{2,1,0:T(8,128)(2,1)S(1)} all-to-all(s16[8,88,128]{2,1,0:T(8,128)(2,1)S(1)} %mix_back.1), channel_id=1, replica_groups=mesh['chan'=8,'blk'=4] {'chan'}, dimensions={0} | all-to-all | bytes 360448 | tf_op jit(solution)/shard_map/all_to_all | solution.py:527
  119.9 1.9 %kernel_finish.1 = f32[144,576]{1,0:T(8,128)} custom-call(s16[8,88,128]{2,1,0:T(8,128)(2,1)S(1)} %all_to_all.32.recv, f32[144,576]{1,0:T(8,128)} %bitcast.8, f32[144,640]{1,0:T(8,128)S(1)} %copy-done.4, f32[144,576]{1,0:T(8,128)S(1)} %kernel_second_pair.1.second, s32[1]{0:T(128)S(6)} %copy.10.size, s32[1]{0:T(128)} %bitcast.2.blk), custom_call_target="tpu_custom_call" | custom-call | flops 4976640000 | tf_op jit(solution)/shard_map/kernel_finish/pallas_call | solution.py:470
  (32 shorter events, 0.1 us)
Async XLA Ops:
  0.0 14.5 %copy-start = (f32[8,8]{1,0:T(8,128)S(1)}, f32[8,8]{1,0:T(8,128)}, u32[]{:S(2)}) copy-start(f32[8,8]{1,0:T(8,128)} %param.16) | copy-start | bytes 772
  2.8 0.7 copy-start.5
  3.4 0.7 copy-start.10
  4.1 25.9 %collective-permute-start.1 = (bf16[144,1152]{1,0:T(8,128)(2,1)S(1)}, bf16[144,1152]{1,0:T(8,128)(2,1)S(1)}, u32[]{:S(2)}, u32[]{:S(2)}) collective-permute-start(bf16[144,1152]{1,0:T(8,128)(2,1)S(1)} %get-tuple-element.40.refs_0_), channel_id=1, source_target_pairs={{0,1},{1,0},{2,3},{3,2},{4,5},{5,4},{6,7},{7,6},{8,9},{9,8},{10,11... | collective-permute-start | bytes 995336 | tf_op jit(solution)/shard_map/ppermute | solution.py:509
  4.6 11.0 %collective-permute-start = (bf16[144,1152]{1,0:T(8,128)(2,1)S(1)}, bf16[144,1152]{1,0:T(8,128)(2,1)S(1)}, u32[]{:S(2)}, u32[]{:S(2)}) collective-permute-start(bf16[144,1152]{1,0:T(8,128)(2,1)S(1)} %get-tuple-element.40.refs_0_), channel_id=1, source_target_pairs={{0,2},{1,3},{2,0},{3,1},{4,6},{5,7},{6,4},{7,5},{8,10},{9,11},{10,... | collective-permute-start | bytes 995336 | tf_op jit(solution)/shard_map/ppermute | solution.py:509
  7.1 5.9 %copy-start.12 = (s32[576]{0:T(1024)S(1)}, s32[576]{0:T(1024)}, u32[]{:S(2)}) copy-start(s32[576]{0:T(1024)} %param.17) | copy-start | bytes 6916
  7.1 17.3 %all-to-all-start = ((s16[8,176,128]{2,1,0:T(8,128)(2,1)}), s16[8,176,128]{2,1,0:T(8,128)(2,1)S(1)}, u32[]{:S(2)}, u32[]{:S(2)}) async-start(s16[8,176,128]{2,1,0:T(8,128)(2,1)} %get-tuple-element.37), calls=%async_computation | async-start | bytes 720896 | tf_op jit(solution)/shard_map/all_to_all | solution.py:527
  13.1 0.7 copy-start.1
  13.7 0.8 copy-start.13
  14.6 0.7 copy-start.14
  24.4 5.6 %collective-permute-start.2 = (bf16[144,1152]{1,0:T(8,128)(2,1)S(1)}, bf16[144,1152]{1,0:T(8,128)(2,1)S(1)}, u32[]{:S(2)}, u32[]{:S(2)}) collective-permute-start(bf16[144,1152]{1,0:T(8,128)(2,1)S(1)} %collective-permute-done.refs_2_), channel_id=1, source_target_pairs={{0,1},{1,0},{2,3},{3,2},{4,5},{5,4},{6,7},{7,6},{8,9},{9,8},{10,11... | collective-permute-start | bytes 995336 | tf_op jit(solution)/shard_map/ppermute | solution.py:509
  26.3 15.3 %all-to-all-start.1 = ((s16[8,176,128]{2,1,0:T(8,128)(2,1)}), s16[8,176,128]{2,1,0:T(8,128)(2,1)S(1)}, u32[]{:S(2)}, u32[]{:S(2)}) async-start(s16[8,176,128]{2,1,0:T(8,128)(2,1)} %mix_cross.1), calls=%async_computation.1 | async-start | bytes 720896 | tf_op jit(solution)/shard_map/all_to_all | solution.py:527
  30.0 0.9 copy-start.6
  30.9 0.9 copy-start.11
  41.9 9.1 %collective-permute-start.4 = (bf16[144,1152]{1,0:T(8,128)(2,1)S(1)}, bf16[144,1152]{1,0:T(8,128)(2,1)S(1)}, u32[]{:S(2)}, u32[]{:S(2)}) collective-permute-start(bf16[144,1152]{1,0:T(8,128)(2,1)S(1)} %get-tuple-element.56.refs_0_), channel_id=1, source_target_pairs={{0,2},{1,3},{2,0},{3,1},{4,6},{5,7},{6,4},{7,5},{8,10},{9,11},{10,... | collective-permute-start | bytes 995336 | tf_op jit(solution)/shard_map/ppermute | solution.py:509
  42.4 9.1 %collective-permute-start.3 = (bf16[144,1152]{1,0:T(8,128)(2,1)S(1)}, bf16[144,1152]{1,0:T(8,128)(2,1)S(1)}, u32[]{:S(2)}, u32[]{:S(2)}) collective-permute-start(bf16[144,1152]{1,0:T(8,128)(2,1)S(1)} %get-tuple-element.56.refs_0_), channel_id=1, source_target_pairs={{0,1},{1,0},{2,3},{3,2},{4,5},{5,4},{6,7},{7,6},{8,9},{9,8},{10,11... | collective-permute-start | bytes 995336 | tf_op jit(solution)/shard_map/ppermute | solution.py:509
  51.0 1.6 %collective-permute-start.5 = (bf16[144,1152]{1,0:T(8,128)(2,1)S(1)}, bf16[144,1152]{1,0:T(8,128)(2,1)S(1)}, u32[]{:S(2)}, u32[]{:S(2)}) collective-permute-start(bf16[144,1152]{1,0:T(8,128)(2,1)S(1)} %collective-permute-done.4.refs_2_), channel_id=1, source_target_pairs={{0,1},{1,0},{2,3},{3,2},{4,5},{5,4},{6,7},{7,6},{8,9},{9,8},{10,11... | collective-permute-start | bytes 995336 | tf_op jit(solution)/shard_map/ppermute | solution.py:509
  70.6 14.3 %copy-start.2 = (f32[1,576]{1,0:T(1,128)S(1)}, f32[1,576]{1,0:T(1,128)}, u32[]{:S(2)}) copy-start(f32[1,576]{1,0:T(1,128)} %occ.5) | copy-start | bytes 6916
  85.2 0.7 copy-start.3
  85.9 7.8 %copy-start.8 = (bf16[144,576]{1,0:T(8,128)(2,1)}, bf16[144,576]{1,0:T(8,128)(2,1)S(1)}, u32[]{:S(2)}) copy-start(bf16[144,576]{1,0:T(8,128)(2,1)S(1)} %get-tuple-element.63.left_eta) | copy-start | bytes 497668
  85.9 7.5 %collective-permute-start.7 = (bf16[144,576]{1,0:T(8,128)(2,1)S(1)}, bf16[144,576]{1,0:T(8,128)(2,1)S(1)}, u32[]{:S(2)}, u32[]{:S(2)}) collective-permute-start(bf16[144,576]{1,0:T(8,128)(2,1)S(1)} %get-tuple-element.60.refs_0_), channel_id=1, source_target_pairs={{0,2},{1,3},{2,0},{3,1},{4,6},{5,7},{6,4},{7,5},{8,10},{9,11},{10,... | collective-permute-start | bytes 497672 | tf_op jit(solution)/shard_map/ppermute | solution.py:509
  86.4 7.3 %collective-permute-start.6 = (bf16[144,576]{1,0:T(8,128)(2,1)S(1)}, bf16[144,576]{1,0:T(8,128)(2,1)S(1)}, u32[]{:S(2)}, u32[]{:S(2)}) collective-permute-start(bf16[144,576]{1,0:T(8,128)(2,1)S(1)} %get-tuple-element.60.refs_0_), channel_id=1, source_target_pairs={{0,1},{1,0},{2,3},{3,2},{4,5},{5,4},{6,7},{7,6},{8,9},{9,8},{10,11... | collective-permute-start | bytes 497672 | tf_op jit(solution)/shard_map/ppermute | solution.py:509
  86.4 13.3 %collective-permute-start.10 = (bf16[144,576]{1,0:T(8,128)(2,1)S(1)}, bf16[144,576]{1,0:T(8,128)(2,1)S(1)}, u32[]{:S(2)}, u32[]{:S(2)}) collective-permute-start(bf16[144,576]{1,0:T(8,128)(2,1)S(1)} %get-tuple-element.61.refs_0_), channel_id=1, source_target_pairs={{0,1},{1,0},{2,3},{3,2},{4,5},{5,4},{6,7},{7,6},{8,9},{9,8},{10,11... | collective-permute-start | bytes 497672 | tf_op jit(solution)/shard_map/ppermute | solution.py:509
  86.9 9.3 %collective-permute-start.9 = (bf16[144,576]{1,0:T(8,128)(2,1)S(1)}, bf16[144,576]{1,0:T(8,128)(2,1)S(1)}, u32[]{:S(2)}, u32[]{:S(2)}) collective-permute-start(bf16[144,576]{1,0:T(8,128)(2,1)S(1)} %get-tuple-element.61.refs_0_), channel_id=1, source_target_pairs={{0,2},{1,3},{2,0},{3,1},{4,6},{5,7},{6,4},{7,5},{8,10},{9,11},{10,... | collective-permute-start | bytes 497672 | tf_op jit(solution)/shard_map/ppermute | solution.py:509
  93.4 1.4 %collective-permute-start.8 = (bf16[144,576]{1,0:T(8,128)(2,1)S(1)}, bf16[144,576]{1,0:T(8,128)(2,1)S(1)}, u32[]{:S(2)}, u32[]{:S(2)}) collective-permute-start(bf16[144,576]{1,0:T(8,128)(2,1)S(1)} %collective-permute-done.7.refs_2_), channel_id=1, source_target_pairs={{0,1},{1,0},{2,3},{3,2},{4,5},{5,4},{6,7},{7,6},{8,9},{9,8},{10,11... | collective-permute-start | bytes 497672 | tf_op jit(solution)/shard_map/ppermute | solution.py:509
  94.8 5.0 %copy-start.9 = (bf16[144,576]{1,0:T(8,128)(2,1)S(1)}, bf16[144,576]{1,0:T(8,128)(2,1)}, u32[]{:S(2)}) copy-start(bf16[144,576]{1,0:T(8,128)(2,1)} %copy-done.8) | copy-start | bytes 497668
  96.2 3.6 %copy-start.7 = (bf16[144,576]{1,0:T(8,128)(2,1)S(1)}, bf16[144,576]{1,0:T(8,128)(2,1)}, u32[]{:S(2)}) copy-start(bf16[144,576]{1,0:T(8,128)(2,1)} %copy-done.5) | copy-start | bytes 497668
  96.2 3.5 %collective-permute-start.11 = (bf16[144,576]{1,0:T(8,128)(2,1)S(1)}, bf16[144,576]{1,0:T(8,128)(2,1)S(1)}, u32[]{:S(2)}, u32[]{:S(2)}) collective-permute-start(bf16[144,576]{1,0:T(8,128)(2,1)S(1)} %collective-permute-done.9.refs_2_), channel_id=1, source_target_pairs={{0,1},{1,0},{2,3},{3,2},{4,5},{5,4},{6,7},{7,6},{8,9},{9,8},{10,11... | collective-permute-start | bytes 497672 | tf_op jit(solution)/shard_map/ppermute | solution.py:509
  96.4 11.9 %all-to-all-start.4 = ((s16[8,88,128]{2,1,0:T(8,128)(2,1)}), s16[8,88,128]{2,1,0:T(8,128)(2,1)S(1)}, u32[]{:S(2)}, u32[]{:S(2)}) async-start(s16[8,88,128]{2,1,0:T(8,128)(2,1)} %kernel_second_cross.1), calls=%async_computation.4 | async-start | bytes 360448 | tf_op jit(solution)/shard_map/all_to_all | solution.py:527
  100.4 19.5 %copy-start.4 = (f32[144,640]{1,0:T(8,128)S(1)}, f32[144,640]{1,0:T(8,128)}, u32[]{:S(2)}) copy-start(f32[144,640]{1,0:T(8,128)} %copy-done.3) | copy-start | bytes 1105924

commit v3 on v2

--- a/solution.py
+++ b/solution.py
@@ -187,7 +187,7 @@
     put_extra(plan, second_ref, extras, 4)
 
 
-def encode_single(plan, values, extra, out_ref, chunk):
+def encode_single(values, extra, out_ref, chunk):
     peak = jnp.maximum(largest(values), jnp.abs(extra))
     e = exponent_of(jnp.maximum(peak, turn(peak, 4)))
     up = scale_up(e)
@@ -197,27 +197,33 @@
         out_ref[chunk, 8 * p : 8 * (p + len(part)), :] = to_int(jnp.concatenate(part, axis=0))
 
 
-def decode_single(plan, in_ref, chunk):
+def single_tiles(plan, in_ref, chunk, scale):
+    values = []
+    for p in range(0, plan.slots, 2):
+        n = min(2, plan.slots - p)
+        rows = from_int(in_ref[chunk, 8 * p : 8 * (p + n), :])
+        values += [rows[8 * q : 8 * q + 8] * scale for q in range(n)]
+    return values
+
+
+def single_scale(plan, in_ref, chunk):
     rows = from_int(in_ref[chunk, 8 * plan.slots : 8 * plan.slots + 8, :])
     down = scale_down(lower(rows))
-    values = []
-    for p in range(plan.slots):
-        values.append(from_int(in_ref[chunk, 8 * p : 8 * p + 8, :]) * down)
-    return values, rows * down
+    return down, rows * down
 
 
 def pack_single(plan, ref, out_ref):
     for chunk in range(plan.chan):
         values = [plan.load(ref, chunk * plan.slots + p) for p in range(plan.slots)]
-        encode_single(plan, values, take_extra(plan, ref, chunk, 4), out_ref, chunk)
+        encode_single(values, take_extra(plan, ref, chunk, 4), out_ref, chunk)
 
 
 def unpack_single(plan, in_ref, ref):
     extras = []
     for chunk in range(plan.chan):
-        values, extra = decode_single(plan, in_ref, chunk)
+        down, extra = single_scale(plan, in_ref, chunk)
         extras.append(extra)
-        for p, value in enumerate(values):
+        for p, value in enumerate(single_tiles(plan, in_ref, chunk, down)):
             plan.store(ref, chunk * plan.slots + p, value)
     put_extra(plan, ref, extras, 4)
 
@@ -242,7 +248,7 @@
     return jnp.dot(a, b, preferred_element_type=f32)
 
 
-def product(plan, left, right_ref, second, main_ref, tail):
+def product(plan, left, right_ref, second):
     m = plan.main
     at = m if second else 0
     main = dot(left, right_ref[:, at : at + m])
@@ -253,8 +259,8 @@
 
 
 def commute(plan, left, right_ref, right_second, other_left, other_ref, other_second, out_ref):
-    a, a_tail = product(plan, left, right_ref, right_second, None, None)
-    b, b_tail = product(plan, other_left, other_ref, other_second, None, None)
+    a, a_tail = product(plan, left, right_ref, right_second)
+    b, b_tail = product(plan, other_left, other_ref, other_second)
     out_ref[:, 0 : plan.main] = a - b
     if plan.tail:
         out_ref[:, plan.main : plan.wide] = a_tail - b_tail
@@ -267,7 +273,14 @@
     return (row < size[0]) & (col < size[0])
 
 
-def kernel_enter(plan, omega, ham, occ, size, blk, send, packed, left_gen, left_ham, gen_s, ham_s):
+def kernel_enter(plan, omega, ham, size, blk, send, gen_s, ham_s):
+    inside = inside_of(plan, size, blk)
+    gen_s[:, 0 : plan.width] = jnp.where(inside, omega[...], 0.0)
+    ham_s[:, 0 : plan.width] = jnp.where(inside, ham[...], 0.0)
+    pack_pair(plan, gen_s, ham_s, send)
+
+
+def kernel_pair_rows(plan, omega, ham, occ, size, blk, packed, left_gen, left_ham, gen_s, ham_s):
     inside = inside_of(plan, size, blk)
     gen = jnp.where(inside, omega[...], 0.0)
     start = jnp.where(inside, ham[...], 0.0)
@@ -275,15 +288,17 @@
     ham_s[:, 0 : plan.width] = start
     left_gen[...] = (gen * occ[...]).astype(bf16)
     left_ham[...] = (start * occ[...]).astype(bf16)
-    pack_pair(plan, gen_s, ham_s, send)
     store_packed(plan, gen_s, ham_s, packed)
 
 
-def kernel_prepare(plan, column_map, occ, select, moved_occ):
+def selection(plan, column_map):
+    rows = lax.broadcasted_iota(jnp.int32, (plan.width, plan.width), 0)
+    return (rows == column_map[...]).astype(f32).astype(bf16)
+
+
+def kernel_prepare(plan, column_map, occ, moved_occ):
     w = plan.width
-    rows = lax.broadcasted_iota(jnp.int32, (w, w), 0)
-    hot = (rows == column_map[...]).astype(f32).astype(bf16)
-    select[...] = hot
+    hot = selection(plan, column_map)
     value = occ[...]
     high = value.astype(bf16)
     rest = value - high.astype(f32)
@@ -314,38 +329,37 @@
         kept[:, m:] = right[:, 2 * m :]
 
 
-def kernel_cross_left(plan, scaled_gen, scaled_ham, select, cross_gen, cross_ham):
-    cross_gen[...] = dot(scaled_gen[...], select[...]).astype(bf16)
-    cross_ham[...] = dot(scaled_ham[...], select[...]).astype(bf16)
+def kernel_cross_left(plan, scaled_gen, scaled_ham, column_map, cross_gen, cross_ham):
+    select = selection(plan, column_map)
+    cross_gen[...] = dot(scaled_gen[...], select).astype(bf16)
+    cross_ham[...] = dot(scaled_ham[...], select).astype(bf16)
 
 
 def kernel_first_pair(plan, left_gen, left_ham, blk, *refs):
-    pieces, (right_gen, first, right) = refs[: plan.blk], refs[plan.blk :]
+    pieces, (right_gen, first, send, right) = refs[: plan.blk], refs[plan.blk :]
     assemble(plan, pieces, blk, right)
     commute(plan, left_gen[...], right, True, left_ham[...], right, False, first)
     keep_first(plan, right, right_gen)
-
-
-def kernel_first_cross(plan, left_gen, left_ham, first, blk, *refs):
+    pack_single(plan, first, send)
+
+
+def kernel_first_cross(plan, left_gen, left_ham, blk, *refs):
     pieces, (right_gen, send, right, cross_s) = refs[: plan.blk], refs[plan.blk :]
     assemble(plan, pieces, blk, right)
     commute(plan, left_gen[...], right, True, left_ham[...], right, False, cross_s)
     keep_first(plan, right, right_gen)
-    pack_pair(plan, cross_s, first, send)
-
-
-def kernel_unpack_eta(plan, recv, first, occ, moved_occ, cross_rows, eta_rows, eta, left_eta, scaled_cross, cross):
+    pack_single(plan, cross_s, send)
+
+
+def kernel_unpack_second(plan, recv, moved_occ, rows, scaled, cross):
     w = plan.width
-    unpack_pair(plan, recv, eta, cross)
-    eta[...] = eta[...] + first[...]
-    cross_rows[...] = cross[:, 0:w].astype(bf16)
-    eta_rows[...] = eta[:, 0:w].astype(bf16)
-    left_eta[...] = (eta[:, 0:w] * occ[...]).astype(bf16)
-    scaled_cross[...] = (cross[:, 0:w] * moved_occ[...]).astype(bf16)
-
-
-def kernel_eta_left(plan, scaled_cross, select, left_cross):
-    left_cross[...] = dot(scaled_cross[...], select[...]).astype(bf16)
+    unpack_single(plan, recv, cross)
+    rows[...] = cross[:, 0:w].astype(bf16)
+    scaled[...] = (cross[:, 0:w] * moved_occ[...]).astype(bf16)
+
+
+def kernel_eta_left(plan, scaled_cross, column_map, left_cross):
+    left_cross[...] = dot(scaled_cross[...], selection(plan, column_map)).astype(bf16)
 
 
 def kernel_second_cross(plan, left_gen, left_eta, right_gen, blk, *refs):
@@ -356,16 +370,22 @@
     pack_single(plan, cross_s, send)
 
 
-def kernel_second_pair(plan, left_gen, left_eta, right_gen, blk, *refs):
-    pieces, (second, right) = refs[: plan.blk], refs[plan.blk :]
+def kernel_eta(plan, recv, first, occ, rows, eta, left_eta, back_s):
+    w = plan.width
+    unpack_single(plan, recv, back_s)
+    value = back_s[:, 0:w] + first[:, 0:w]
+    eta[...] = value
+    rows[...] = value.astype(bf16)
+    left_eta[...] = (value * occ[...]).astype(bf16)
+
+
+def kernel_finish(plan, recv, ham, eta, left_gen, left_eta, right_gen, size, blk, *refs):
+    pieces, (out, right, back_s) = refs[: plan.blk], refs[plan.blk :]
+    w = plan.width
     assemble(plan, pieces, blk, right)
-    second[...] = dot(left_gen[...], right[...]) - dot(left_eta[...], right_gen[:, 0 : plan.width])
-
-
-def kernel_finish(plan, recv, ham, eta, second, size, blk, out, back_s):
+    second = dot(left_gen[...], right[...]) - dot(left_eta[...], right_gen[:, 0:w])
     unpack_single(plan, recv, back_s)
-    w = plan.width
-    total = ham[...] + eta[:, 0:w] + 0.5 * (second[...] + back_s[:, 0:w])
+    total = ham[...] + eta[...] + 0.5 * (second + back_s[:, 0:w])
     out[...] = jnp.where(inside_of(plan, size, blk), total, 0.0)
 
 
@@ -373,33 +393,18 @@
     n = len(values)
     out = []
     for k in range(n):
-        terms = [values[c] * (mixing[c, k] if transposed else mixing[k, c]) for c in range(n)]
+        rows = [c * n + k if transposed else k * n + c for c in range(n)]
+        terms = [value * mixing[pl.ds(r, value.shape[0], stride=0), :] for r, value in zip(rows, values)]
         out.append(functools.reduce(jnp.add, terms))
     return out
 
 
-def both_of(mixing, first, second):
-    restored = mixed(mixing, first, True)
-    crossed = mixed(mixing, [v + r for v, r in zip(second, restored)], False)
-    return restored, crossed
-
-
-def kernel_mix_pair(plan, both, mixing, recv, send, kept):
+def kernel_mix_cross(plan, mixing, recv, send, kept):
     n = plan.chan
     scales = [pair_scale(plan, recv, c) for c in range(n)]
-    extra = [s[1] for s in scales]
-    if both:
-        restored, crossed = both_of(mixing, extra, [turn(x, 4) for x in extra])
-        extra = [jnp.where(sublane() < 4, r, turn(x, 4)) for r, x in zip(restored, crossed)]
-    else:
-        extra = mixed(mixing, extra, False)
+    extra = mixed(mixing, [s[1] for s in scales], False)
     for p in range(plan.slots):
-        values = [from_int(recv[c, 16 * p : 16 * p + 16, :]) * scales[c][0] for c in range(n)]
-        if both:
-            pairs = zip(*both_of(mixing, [v[0:8] for v in values], [v[8:16] for v in values]))
-            result = [jnp.concatenate(pair, axis=0) for pair in pairs]
-        else:
-            result = mixed(mixing, values, False)
+        result = mixed(mixing, [from_int(recv[c, 16 * p : 16 * p + 16, :]) * scales[c][0] for c in range(n)], False)
         for k in range(n):
             kept[k, 16 * p : 16 * p + 16, :] = result[k]
     for k in range(n):
@@ -407,57 +412,83 @@
         encode_pair(plan, values, extra[k], write_pair(send, k))
 
 
-def kernel_mix_single(plan, both, mixing, recv, send, kept):
-    n = plan.chan
-    downs, extra = [], []
-    for c in range(n):
-        rows = from_int(recv[c, 8 * plan.slots : 8 * plan.slots + 8, :])
-        downs.append(scale_down(lower(rows)))
-        extra.append(rows * downs[c])
-    extra = mixed(mixing, extra, True)
-    for p in range(plan.slots):
-        result = mixed(mixing, [from_int(recv[c, 8 * p : 8 * p + 8, :]) * downs[c] for c in range(n)], True)
-        for k in range(n):
-            kept[k, 8 * p : 8 * p + 8, :] = result[k]
-    for k in range(n):
+def scales_of(plan, recv):
+    found = [single_scale(plan, recv, c) for c in range(plan.chan)]
+    return [f[0] for f in found], [f[1] for f in found]
+
+
+def groups_of(plan):
+    return [(p, min(2, plan.slots - p)) for p in range(0, plan.slots, 2)]
+
+
+def tiles_of(plan, recv, scales, p, n):
+    wide = [jnp.concatenate([x] * n, axis=0) for x in scales]
+    return [from_int(recv[c, 8 * p : 8 * (p + n), :]) * wide[c] for c in range(plan.chan)]
+
+
+def encode_all(plan, kept, extra, send):
+    for k in range(plan.chan):
         values = [kept[k, 8 * p : 8 * p + 8, :] for p in range(plan.slots)]
-        encode_single(plan, values, extra[k], send, k)
-
-
-def plain_mix(plan, kind, mixing, recv):
+        encode_single(values, extra[k], send, k)
+
+
+def kernel_mix_back(plan, mixing, recv, send, kept):
+    scales, extra = scales_of(plan, recv)
+    for p, n in groups_of(plan):
+        for k, value in enumerate(mixed(mixing, tiles_of(plan, recv, scales, p, n), True)):
+            kept[k, 8 * p : 8 * (p + n), :] = value
+    encode_all(plan, kept, mixed(mixing, extra, True), send)
+
+
+def kernel_mix_both(plan, mixing, recv, recv_first, send, send_back, kept, kept_back):
+    scales, extra = scales_of(plan, recv)
+    scales_first, extra_first = scales_of(plan, recv_first)
+
+    def both(value, first):
+        back = mixed(mixing, value, True)
+        return back, mixed(mixing, [f + r for f, r in zip(first, back)], False)
+
+    for p, n in groups_of(plan):
+        back, cross = both(tiles_of(plan, recv, scales, p, n), tiles_of(plan, recv_first, scales_first, p, n))
+        for k in range(plan.chan):
+            kept_back[k, 8 * p : 8 * (p + n), :] = back[k]
+            kept[k, 8 * p : 8 * (p + n), :] = cross[k]
+    extra_back, extra = both(extra, extra_first)
+    encode_all(plan, kept, extra, send)
+    encode_all(plan, kept_back, extra_back, send_back)
+
+
+def plain_mix(plan, kind, mixing, recv, recv_first=None):
     n, slots = plan.chan, plan.slots
+    high = 16 if kind == "cross" else 8
 
     def mix(spec, value):
         return jnp.einsum(spec, mixing, value, precision=exact_mode, preferred_element_type=f32)
 
     def spread_rows(e):
-        if kind == "back":
-            return jnp.concatenate([e[:, 0:4]] * 2, axis=1)
-        return jnp.concatenate([e[:, 0:4]] * 2 + [e[:, 4:8]] * 2, axis=1)
-
-    raw = recv.astype(jnp.int32).astype(f32)
-    high = 8 if kind == "back" else 16
-    e = raw[:, high * slots : high * slots + 8]
-    body = raw[:, 0 : high * slots].reshape(n, slots, high, 128) * scale_down(spread_rows(e))[:, None]
+        if kind == "cross":
+            return jnp.concatenate([e[:, 0:4]] * 2 + [e[:, 4:8]] * 2, axis=1)
+        return jnp.concatenate([e[:, 0:4]] * 2, axis=1)
+
+    def decode(chunks):
+        raw = chunks.astype(jnp.int32).astype(f32)
+        e = raw[:, high * slots : high * slots + 8]
+        return raw[:, 0 : high * slots].reshape(n, slots, high, 128) * scale_down(spread_rows(e))[:, None]
+
+    def encode(value):
+        peak = jnp.max(jnp.abs(value), axis=1)
+        peak = jnp.max(peak.reshape(n, high // 8, 2, 4, 128), axis=2).reshape(n, high // 2, 128)
+        e = exponent_of(peak)
+        scaled = value * scale_up(spread_rows(e))[:, None]
+        out = jnp.concatenate([scaled.reshape(n, -1, 128), e], axis=1)
+        return to_int(jnp.pad(out, ((0, 0), (0, recv.shape[1] - out.shape[1]), (0, 0))))
+
     if kind == "cross":
-        result = mix("kc,cpsl->kpsl", body)
-    elif kind == "both":
-        restored = mix("ck,cpsl->kpsl", body[:, :, 0:8])
-        crossed = mix("kc,cpsl->kpsl", body[:, :, 8:16] + restored)
-        result = jnp.concatenate([restored, crossed], axis=2)
-    else:
-        result = mix("ck,cpsl->kpsl", body)
-    peak = jnp.max(jnp.abs(result), axis=1)
-    peak = jnp.max(peak.reshape(n, high // 8, 2, 4, 128), axis=2).reshape(n, high // 2, 128)
-    e = exponent_of(peak)
-    scaled = result * scale_up(spread_rows(e))[:, None]
-    out = jnp.concatenate([scaled.reshape(n, -1, 128), e], axis=1)
-    out = jnp.pad(out, ((0, 0), (0, recv.shape[1] - out.shape[1]), (0, 0)))
-    return to_int(out)
-
-
-def near(value):
-    return pltpu.with_memory_space_constraint(value, pltpu.VMEM)
+        return encode(mix("kc,cpsl->kpsl", decode(recv)))
+    back = mix("ck,cpsl->kpsl", decode(recv))
+    if kind == "back":
+        return encode(back)
+    return encode(mix("kc,cpsl->kpsl", decode(recv_first) + back)), encode(back)
 
 
 def call(body, plan, outs, specs, scratch=(), flops=0, final=False):
@@ -473,7 +504,6 @@
             in_specs=[smem() if s == "s" else vmem() for s in specs],
             out_specs=tuple(vmem() for _ in outs),
             scratch_shapes=tuple(pltpu.VMEM(s, d) for s, d in scratch),
-            name=body.__name__,
             cost_estimate=pl.CostEstimate(flops=flops or plan.rows * plan.width * 60000, transcendentals=0, bytes_accessed=0),
             compiler_params=pltpu.CompilerParams(vmem_limit_bytes=GRANT),
         )(*placed)
@@ -481,19 +511,21 @@
     return run
 
 
-def mix_call(plan, kind, mixing, recv):
+MIXERS = {"cross": kernel_mix_cross, "both": kernel_mix_both, "back": kernel_mix_back}
+
+
+def mix_call(plan, kind, mixing, *recv):
     if plan.chan > UNROLLED:
-        return plain_mix(plan, kind, mixing, recv)
-    body = kernel_mix_single if kind == "back" else kernel_mix_pair
-    return pl.pallas_call(
-        functools.partial(body, plan, kind == "both"),
-        out_shape=pltpu.VMEM(recv.shape, i16),
-        in_specs=[smem(), vmem()],
-        out_specs=vmem(),
-        scratch_shapes=(pltpu.VMEM((plan.chan, recv.shape[1], 128), f32),),
-        name="mix_" + kind,
-        compiler_params=pltpu.CompilerParams(vmem_limit_bytes=GRANT),
-    )(mixing, near(recv))
+        return plain_mix(plan, kind, mixing, *recv)
+    rows = recv[0].shape[1]
+    outs = call(
+        MIXERS[kind],
+        plan,
+        [((plan.chan, rows, 128), i16)] * len(recv),
+        "v" * (1 + len(recv)),
+        [((plan.chan, rows, 128), f32)] * len(recv),
+    )(mixing, *recv)
+    return outs if len(recv) > 1 else outs[0]
 
 
 def mixing_matrix(jlabel, family, sixj):
@@ -545,51 +577,63 @@
     right_kept = ((rows * blk, plan.wide), bf16)
     right_one = ((rows * blk, width), bf16)
 
-    send, pair_rows, left_gen, left_ham = call(
-        kernel_enter, plan, [pair, packed, left, left], "hhhss", [wide, wide]
-    )(omega, ham, pair_occ, block_size, blk_index)
-    select, moved_occ = call(kernel_prepare, plan, [((width, width), bf16), ((1, width), f32)], "vv")(
-        column_map.reshape(1, width), cross_occ
+    (send,) = call(kernel_enter, plan, [pair], "hhss", [wide, wide])(omega, ham, block_size, blk_index)
+    pair_rows, left_gen, left_ham = call(kernel_pair_rows, plan, [packed, left, left], "hhhss", [wide, wide])(
+        omega, ham, pair_occ, block_size, blk_index
     )
+    column_row = column_map.reshape(1, width)
+    (moved_occ,) = call(kernel_prepare, plan, [((1, width), f32)], "vv")(column_row, cross_occ)
     mixing = mixing_matrix(jlabel, family, sixj)
+    if chan <= UNROLLED:
+        mixing = jnp.broadcast_to(mixing.reshape(chan * chan, 1), (chan * chan, 128))
     pair_far = far_rows(pair_rows, blk)
     recv = exchange(send)
-    recv, mixing, select, moved_occ, pair_far = lax.optimization_barrier((recv, mixing, select, moved_occ, pair_far))
+    recv, mixing, moved_occ = lax.optimization_barrier((recv, mixing, moved_occ))
+
     pair_pieces = near_rows(pair_rows, pair_far, blk)
     recv = exchange(mix_call(plan, "cross", mixing, recv))
-    pair_right, first = call(kernel_first_pair, plan, [right_kept, wide], "vvs" + "v" * blk, [right])(
-        left_gen, left_ham, blk_index, *pair_pieces
-    )
-    recv, pair_right, first = lax.optimization_barrier((recv, pair_right, first))
+    pair_right, first, send_first = call(
+        kernel_first_pair, plan, [right_kept, wide, single], "vvs" + "v" * blk, [right]
+    )(left_gen, left_ham, blk_index, *pair_pieces)
+    recv, pair_right, first, send_first = lax.optimization_barrier((recv, pair_right, first, send_first))
     cross_rows, scaled_gen, scaled_ham = call(
         kernel_unpack_cross, plan, [packed, left, left], "vv", [wide, wide]
     )(recv, moved_occ)
-    cross_pieces = near_rows(cross_rows, far_rows(cross_rows, blk), blk)
-    cross_gen_left, cross_ham_left = call(kernel_cross_left, plan, [left, left], "vvv")(scaled_gen, scaled_ham, select)
+    cross_rows, send_first = lax.optimization_barrier((cross_rows, send_first))
+    cross_far = far_rows(cross_rows, blk)
+    recv_first = exchange(send_first)
+    cross_gen_left, cross_ham_left = call(kernel_cross_left, plan, [left, left], "vvv")(
+        scaled_gen, scaled_ham, column_row
+    )
+    cross_far, cross_gen_left, cross_ham_left = lax.optimization_barrier((cross_far, cross_gen_left, cross_ham_left))
+    cross_pieces = near_rows(cross_rows, cross_far, blk)
     cross_right, send = call(
-        kernel_first_cross, plan, [right_kept, pair], "vvvs" + "v" * blk, [right, wide]
-    )(cross_gen_left, cross_ham_left, first, blk_index, *cross_pieces)
-    recv = exchange(mix_call(plan, "both", mixing, exchange(send)))
-    cross_rows, eta_rows, eta, left_eta, scaled_cross = call(
-        kernel_unpack_eta, plan, [left, left, wide, left, left], "vvvv", [wide]
-    )(recv, first, pair_occ, moved_occ)
-    cross_far = far_rows(cross_rows, blk)
+        kernel_first_cross, plan, [right_kept, single], "vvs" + "v" * blk, [right, wide]
+    )(cross_gen_left, cross_ham_left, blk_index, *cross_pieces)
+    send, recv_first = lax.optimization_barrier((send, recv_first))
+
+    send, send_back = mix_call(plan, "both", mixing, exchange(send), recv_first)
+    recv = exchange(send)
+    recv, send_back = lax.optimization_barrier((recv, send_back))
+    second_rows, scaled = call(kernel_unpack_second, plan, [left, left], "vv", [wide])(recv, moved_occ)
+    second_far = far_rows(second_rows, blk)
+    recv_back = exchange(send_back)
+    (cross_eta_left,) = call(kernel_eta_left, plan, [left], "vv")(scaled, column_row)
+    second_far, cross_eta_left = lax.optimization_barrier((second_far, cross_eta_left))
+    second_pieces = near_rows(second_rows, second_far, blk)
+    (send,) = call(kernel_second_cross, plan, [single], "vvvs" + "v" * blk, [right_one, wide])(
+        cross_gen_left, cross_eta_left, cross_right, blk_index, *second_pieces
+    )
+    send, recv_back = lax.optimization_barrier((send, recv_back))
+
+    recv = exchange(send)
+    eta_rows, eta, left_eta = call(kernel_eta, plan, [left, plain, left], "vvv", [wide])(recv_back, first, pair_occ)
     eta_far = far_rows(eta_rows, blk)
-    cross_pieces = near_rows(cross_rows, cross_far, blk)
-    (cross_eta_left,) = call(kernel_eta_left, plan, [left], "vv")(scaled_cross, select)
-    (send,) = call(kernel_second_cross, plan, [single], "vvvs" + "v" * blk, [right_one, wide])(
-        cross_gen_left, cross_eta_left, cross_right, blk_index, *cross_pieces
-    )
-    send, eta_far = lax.optimization_barrier((send, eta_far))
-    recv = exchange(send)
     eta_pieces = near_rows(eta_rows, eta_far, blk)
-    (second,) = call(kernel_second_pair, plan, [plain], "vvvs" + "v" * blk, [right_one])(
-        left_gen, left_eta, pair_right, blk_index, *eta_pieces
-    )
-    recv, second = lax.optimization_barrier((recv, second))
+    recv, eta_pieces = lax.optimization_barrier((recv, eta_pieces))
     recv = exchange(mix_call(plan, "back", mixing, recv))
-    (out,) = call(kernel_finish, plan, [plain], "vhvvss", [wide], final=True)(
-        recv, ham, eta, second, block_size, blk_index
+    (out,) = call(kernel_finish, plan, [plain], "vvvvvvss" + "v" * blk, [right_one, wide], final=True)(
+        recv, ham, eta, left_gen, left_eta, pair_right, block_size, blk_index, *eta_pieces
     )
     return out[None]
 
@@ -607,6 +651,4 @@
         P(),
     )
     out_specs = P("chan", "blk", None)
-    return jax.shard_map(
-        on_device, mesh=mesh, in_specs=in_specs, out_specs=out_specs, check_vma=False
-    )
+    return jax.shard_map(on_device, mesh=mesh, in_specs=in_specs, out_specs=out_specs, check_vma=False)

time: 123 us -> 129 us (1.049)
  blocking collectives: 40.9 us -> 31 us
  waiting for transfers between devices: 41.7 us -> 50 us
  starting transfers between devices: 19.2 us -> 25.2 us
  local copies, waits for them, and re-layouts: 5.1 us -> 7.41 us
    all_to_all x3, blocking collectives: 40.9 us -> 31 us  [exchange(): return lax.all_to_all(value, 'chan', 0, 0, tiled=True)]
    all_to_all x3 -> x5, waiting for transfers between devices: 25.8 us -> 35.1 us  [exchange(): return lax.all_to_all(value, 'chan', 0, 0, tiled=True)]
    all_to_all x3 -> x5, starting transfers between devices: 13 us -> 20 us  [exchange(): return lax.all_to_all(value, 'chan', 0, 0, tiled=True)]
    pallas_call x3 -> x0, Pallas kernels: 4.12 us -> none  [mix_call(): pl.pallas_call(functools.partial(body, plan, kind == 'both'), out_shape=p...]
    pallas_call x11 -> x15, Pallas kernels: 9.54 us -> 13.4 us  [run(): pl.pallas_call(functools.partial(body, plan), out_shape=tuple(((jax.Shape...]
    unnamed x30 -> x32, local copies, waits for them, and re-layouts: 5.1 us -> 7.25 us
  transfers between devices with their start and end apart: 15 -> 17, of which waited for: 8 -> 8; matrix products, arithmetic and copies ran while one was open for 0% -> 0% of each run, Pallas kernels for 5% -> 7%
where the time goes in v3:
time: 129 us; the launch traced here: 128 us
  waiting for transfers between devices  50 us (39%)
  blocking collectives  31 us (24%)
  starting transfers between devices  25.2 us (20%)
  Pallas kernels  13.4 us (10%)
  local copies, waits for them, and re-layouts  7.41 us (6%)
    all_to_all x5, waiting for transfers between devices, exchange(): return lax.all_to_all(value, 'chan', 0, 0, tiled=True)  35.1 us
    all_to_all x3, blocking collectives, exchange(): return lax.all_to_all(value, 'chan', 0, 0, tiled=True)  31 us
    all_to_all x5, starting transfers between devices, exchange(): return lax.all_to_all(value, 'chan', 0, 0, tiled=True)  20 us
    ppermute x12, waiting for transfers between devices, swap(): return lax.ppermute(value, 'blk', [(b, b ^ bits) for b in range(size)])  14.9 us
    pallas_call x15, Pallas kernels, run(): pl.pallas_call(functools.partial(body, plan), out_shape=tuple(((jax.Shape...  13.4 us
    unnamed x32, local copies, waits for them, and re-layouts  7.25 us
    ppermute x12, starting transfers between devices, swap(): return lax.ppermute(value, 'blk', [(b, b ^ bits) for b in range(size)])  5.26 us
  transfers between devices with their start and end apart: 17, of which 8 were waited for; matrix products, arithmetic and copies ran while one was open for 0% of the time, Pallas kernels for 7%

profile of v3, /device:TPU:0, one launch (start us, length us, event | category | flops | bytes accessed | tf_op | source)
XLA Modules:
  0.0 128.3 jit_solution(4985739549191785659)
XLA Ops:
  0.7 1.3 %shard_map.94 = (bf16[144,1152]{1,0:T(8,128)(2,1)S(1)}, bf16[144,576]{1,0:T(8,128)(2,1)S(1)}, bf16[144,576]{1,0:T(8,128)(2,1)S(1)}) custom-call(f32[144,576]{1,0:T(8,128)} %bitcast.9, f32[144,576]{1,0:T(8,128)} %bitcast.6, f32[1,576]{1,0:T(1,128)} %occ.5, s32[1]{0:T(128)S(6)} %copy.10.size, s32[1]{0:T(128)} %bitcast.2.blk), custom_call_target="tpu_custom_call" | custom-call | flops 4976640000 | tf_op jit(solution)/shard_map/pallas_call | solution.py:501
  2.0 3.1 %collective-permute-start.1 = (bf16[144,1152]{1,0:T(8,128)(2,1)S(1)}, bf16[144,1152]{1,0:T(8,128)(2,1)S(1)}, u32[]{:S(2)}, u32[]{:S(2)}) collective-permute-start(bf16[144,1152]{1,0:T(8,128)(2,1)S(1)} %get-tuple-element.54.refs_0_), channel_id=1, source_target_pairs={{0,2},{1,3},{2,0},{3,1},{4,6},{5,7},{6,4},{7,5},{8,10},{9,11},{10,... | collective-permute-start | bytes 995336 | tf_op jit(solution)/shard_map/ppermute | solution.py:541
  5.0 2.0 %shard_map.91 = s16[8,176,128]{2,1,0:T(8,128)(2,1)} custom-call(f32[144,576]{1,0:T(8,128)} %bitcast.10, f32[144,576]{1,0:T(8,128)} %bitcast.7, s32[1]{0:T(128)S(6)} %copy.10.size, s32[1]{0:T(128)} %bitcast.2.blk), custom_call_target="tpu_custom_call" | custom-call | flops 4976640000 | tf_op jit(solution)/shard_map/pallas_call | solution.py:501
  7.1 5.9 %all-to-all-start = ((s16[8,176,128]{2,1,0:T(8,128)(2,1)}), s16[8,176,128]{2,1,0:T(8,128)(2,1)S(1)}, u32[]{:S(2)}, u32[]{:S(2)}) async-start(s16[8,176,128]{2,1,0:T(8,128)(2,1)} %shard_map.91), calls=%async_computation | async-start | bytes 720896 | tf_op jit(solution)/shard_map/all_to_all | solution.py:559
  13.1 0.6 copy-done.14
  13.7 0.2 fusion
  13.9 0.5 copy-done.15
  14.3 0.2 convolution_select_fusion
  14.6 0.6 copy-done.2
  15.2 0.7 shard_map.92.moved_occ
  15.9 0.3 collective-permute-start.2
  16.2 8.5 %all-to-all-done.recv = s16[8,176,128]{2,1,0:T(8,128)(2,1)S(1)} async-done(((s16[8,176,128]{2,1,0:T(8,128)(2,1)}), s16[8,176,128]{2,1,0:T(8,128)(2,1)S(1)}, u32[]{:S(2)}, u32[]{:S(2)}) %all-to-all-start) | async-done | bytes 360480 | tf_op jit(solution)/shard_map/all_to_all | solution.py:559
  24.7 1.3 %shard_map.93 = s16[8,176,128]{2,1,0:T(8,128)(2,1)} custom-call(f32[64,128]{1,0:T(8,128)S(1)} %broadcast_in_dim.7.mixing, s16[8,176,128]{2,1,0:T(8,128)(2,1)S(1)} %all-to-all-done.recv), custom_call_target="tpu_custom_call" | custom-call | flops 4976640000 | tf_op jit(solution)/shard_map/pallas_call | solution.py:501
  26.0 3.6 %all-to-all-start.1 = ((s16[8,176,128]{2,1,0:T(8,128)(2,1)}), s16[8,176,128]{2,1,0:T(8,128)(2,1)S(1)}, u32[]{:S(2)}, u32[]{:S(2)}) async-start(s16[8,176,128]{2,1,0:T(8,128)(2,1)} %shard_map.93), calls=%async_computation.1 | async-start | bytes 720896 | tf_op jit(solution)/shard_map/all_to_all | solution.py:559
  29.7 1.5 %shard_map.95 = (bf16[576,640]{1,0:T(8,128)(2,1)S(1)}, f32[144,640]{1,0:T(8,128)S(1)}, s16[8,88,128]{2,1,0:T(8,128)(2,1)}) custom-call(bf16[144,576]{1,0:T(8,128)(2,1)S(1)} %get-tuple-element.52.left_gen, bf16[144,576]{1,0:T(8,128)(2,1)S(1)} %get-tuple-element.53.left_ham, s32[1]{0:T(128)} %bitcast.2.blk, bf16[144,1152]{1,0:T(8,128)(2,1)S(1)} %get-tuple-element.54.refs_0_, ...), custom_call_target="tpu_custom_call" | custom-call | flops 4976640000 | tf_op jit(solution)/shard_map/pallas_call | solution.py:501
  31.2 0.7 copy-done.4
  31.9 9.0 %all-to-all-done.1.recv = s16[8,176,128]{2,1,0:T(8,128)(2,1)S(1)} async-done(((s16[8,176,128]{2,1,0:T(8,128)(2,1)}), s16[8,176,128]{2,1,0:T(8,128)(2,1)S(1)}, u32[]{:S(2)}, u32[]{:S(2)}) %all-to-all-start.1) | async-done | bytes 360480 | tf_op jit(solution)/shard_map/all_to_all | solution.py:559
  40.9 0.2 shard_map.96
  41.2 0.6 collective-permute-start.3
  41.7 0.6 shard_map.97
  42.4 0.7 copy-done.6
  43.0 0.7 copy-done.11
  43.7 7.7 %collective-permute-done.3.refs_2_ = bf16[144,1152]{1,0:T(8,128)(2,1)S(1)} collective-permute-done((bf16[144,1152]{1,0:T(8,128)(2,1)S(1)}, bf16[144,1152]{1,0:T(8,128)(2,1)S(1)}, u32[]{:S(2)}, u32[]{:S(2)}) %collective-permute-start.3) | collective-permute-done | bytes 331808 | tf_op jit(solution)/shard_map/ppermute | solution.py:541
  51.4 3.6 %all-to-all-start.2 = ((s16[8,88,128]{2,1,0:T(8,128)(2,1)}), s16[8,88,128]{2,1,0:T(8,128)(2,1)S(1)}, u32[]{:S(2)}, u32[]{:S(2)}) async-start(s16[8,88,128]{2,1,0:T(8,128)(2,1)} %get-tuple-element.71), calls=%async_computation.2 | async-start | bytes 360448 | tf_op jit(solution)/shard_map/all_to_all | solution.py:559
  55.0 0.9 copy-done.7
  56.0 0.9 copy-done.12
  56.9 0.8 shard_map.98
  57.7 5.7 %all-to-all-done.2.recv_first = s16[8,88,128]{2,1,0:T(8,128)(2,1)S(1)} async-done(((s16[8,88,128]{2,1,0:T(8,128)(2,1)}), s16[8,88,128]{2,1,0:T(8,128)(2,1)S(1)}, u32[]{:S(2)}, u32[]{:S(2)}) %all-to-all-start.2) | async-done | bytes 180256 | tf_op jit(solution)/shard_map/all_to_all | solution.py:559
  63.4 10.5 %all_to_all.40.recv = s16[8,88,128]{2,1,0:T(8,128)(2,1)S(1)} all-to-all(s16[8,88,128]{2,1,0:T(8,128)(2,1)S(1)} %get-tuple-element.72), channel_id=1, replica_groups=mesh['chan'=8,'blk'=4] {'chan'}, dimensions={0} | all-to-all | bytes 360448 | tf_op jit(solution)/shard_map/all_to_all | solution.py:559
  73.9 1.3 %shard_map.99 = (s16[8,88,128]{2,1,0:T(8,128)(2,1)S(1)}, s16[8,88,128]{2,1,0:T(8,128)(2,1)}) custom-call(f32[64,128]{1,0:T(8,128)S(1)} %broadcast_in_dim.7.mixing, s16[8,88,128]{2,1,0:T(8,128)(2,1)S(1)} %all_to_all.40.recv, s16[8,88,128]{2,1,0:T(8,128)(2,1)S(1)} %all-to-all-done.2.recv_first), custom_call_target="tpu_custom_call" | custom-call | flops 4976640000 | tf_op jit(solution)/shard_map/pallas_call | solution.py:501
  75.2 10.3 %all_to_all.41.recv = s16[8,88,128]{2,1,0:T(8,128)(2,1)S(1)} all-to-all(s16[8,88,128]{2,1,0:T(8,128)(2,1)S(1)} %get-tuple-element.74), channel_id=1, replica_groups=mesh['chan'=8,'blk'=4] {'chan'}, dimensions={0} | all-to-all | bytes 360448 | tf_op jit(solution)/shard_map/all_to_all | solution.py:559
  85.5 0.1 shard_map.100
  85.7 0.6 collective-permute-start.6
  86.3 0.3 shard_map.101.left_eta
  86.6 0.7 copy-done.9
  87.3 5.4 %collective-permute-done.6.refs_2_ = bf16[144,576]{1,0:T(8,128)(2,1)S(1)} collective-permute-done((bf16[144,576]{1,0:T(8,128)(2,1)S(1)}, bf16[144,576]{1,0:T(8,128)(2,1)S(1)}, u32[]{:S(2)}, u32[]{:S(2)}) %collective-permute-start.6) | collective-permute-done | bytes 165920 | tf_op jit(solution)/shard_map/ppermute | solution.py:541
  92.8 3.4 %all-to-all-start.5 = ((s16[8,88,128]{2,1,0:T(8,128)(2,1)}), s16[8,88,128]{2,1,0:T(8,128)(2,1)S(1)}, u32[]{:S(2)}, u32[]{:S(2)}) async-start(s16[8,88,128]{2,1,0:T(8,128)(2,1)} %get-tuple-element.82), calls=%async_computation.5 | async-start | bytes 360448 | tf_op jit(solution)/shard_map/all_to_all | solution.py:559
  96.2 0.9 copy-done.10
  97.1 1.4 %shard_map.102 = s16[8,88,128]{2,1,0:T(8,128)(2,1)} custom-call(bf16[144,576]{1,0:T(8,128)(2,1)S(1)} %copy-done.8, bf16[144,576]{1,0:T(8,128)(2,1)S(1)} %copy-done.10, bf16[576,640]{1,0:T(8,128)(2,1)S(1)} %get-tuple-element.80.right_gen, s32[1]{0:T(128)} %bitcast.2.blk, bf16[144,576]{1,0:T(8,128)(2,1)S(1)} %get-tuple-element.77.refs_0_, ...), custom_call_target="tpu_custom_call" | custom-call | flops 4976640000 | tf_op jit(solution)/shard_map/pallas_call | solution.py:501
  98.5 6.2 %all-to-all-done.5.recv = s16[8,88,128]{2,1,0:T(8,128)(2,1)S(1)} async-done(((s16[8,88,128]{2,1,0:T(8,128)(2,1)}), s16[8,88,128]{2,1,0:T(8,128)(2,1)S(1)}, u32[]{:S(2)}, u32[]{:S(2)}) %all-to-all-start.5) | async-done | bytes 180256 | tf_op jit(solution)/shard_map/all_to_all | solution.py:559
  104.8 0.1 shard_map.103
  104.9 0.6 collective-permute-start.10
  105.5 3.4 %all-to-all-start.6 = ((s16[8,88,128]{2,1,0:T(8,128)(2,1)}), s16[8,88,128]{2,1,0:T(8,128)(2,1)S(1)}, u32[]{:S(2)}, u32[]{:S(2)}) async-start(s16[8,88,128]{2,1,0:T(8,128)(2,1)} %shard_map.102), calls=%async_computation.6 | async-start | bytes 360448 | tf_op jit(solution)/shard_map/all_to_all | solution.py:559
  108.9 1.7 %collective-permute-done.10.refs_2_ = bf16[144,576]{1,0:T(8,128)(2,1)S(1)} collective-permute-done((bf16[144,576]{1,0:T(8,128)(2,1)S(1)}, bf16[144,576]{1,0:T(8,128)(2,1)S(1)}, u32[]{:S(2)}, u32[]{:S(2)}) %collective-permute-start.10) | collective-permute-done | bytes 165920 | tf_op jit(solution)/shard_map/ppermute | solution.py:541
  110.7 5.8 %all-to-all-done.6.recv = s16[8,88,128]{2,1,0:T(8,128)(2,1)S(1)} async-done(((s16[8,88,128]{2,1,0:T(8,128)(2,1)}), s16[8,88,128]{2,1,0:T(8,128)(2,1)S(1)}, u32[]{:S(2)}, u32[]{:S(2)}) %all-to-all-start.6) | async-done | bytes 180256 | tf_op jit(solution)/shard_map/all_to_all | solution.py:559
  116.5 0.3 shard_map.104
  116.8 10.2 %all_to_all.42.recv = s16[8,88,128]{2,1,0:T(8,128)(2,1)S(1)} all-to-all(s16[8,88,128]{2,1,0:T(8,128)(2,1)S(1)} %shard_map.104), channel_id=1, replica_groups=mesh['chan'=8,'blk'=4] {'chan'}, dimensions={0} | all-to-all | bytes 360448 | tf_op jit(solution)/shard_map/all_to_all | solution.py:559
  127.0 1.3 %shard_map.105 = f32[144,576]{1,0:T(8,128)} custom-call(s16[8,88,128]{2,1,0:T(8,128)(2,1)S(1)} %all_to_all.42.recv, f32[144,576]{1,0:T(8,128)S(1)} %bitcast.8, f32[144,576]{1,0:T(8,128)S(1)} %get-tuple-element.88.eta, bf16[144,576]{1,0:T(8,128)(2,1)S(1)} %get-tuple-element.52.left_gen, bf16[144,576]{1,0:T(8,128)(2,1)S(1)} %get-tuple-element.89.left_eta, ...), custom_call_target="tpu_custom_call" | custom-call | flops 4976640000 | tf_op jit(solution)/shard_map/pallas_call | solution.py:501
  (41 shorter events, 0.4 us)
Async XLA Ops:
  0.0 13.0 %copy-start = (f32[8,8]{1,0:T(8,128)S(1)}, f32[8,8]{1,0:T(8,128)}, u32[]{:S(2)}) copy-start(f32[8,8]{1,0:T(8,128)} %param.16) | copy-start | bytes 772
  2.0 13.9 %collective-permute-start.1 = (bf16[144,1152]{1,0:T(8,128)(2,1)S(1)}, bf16[144,1152]{1,0:T(8,128)(2,1)S(1)}, u32[]{:S(2)}, u32[]{:S(2)}) collective-permute-start(bf16[144,1152]{1,0:T(8,128)(2,1)S(1)} %get-tuple-element.54.refs_0_), channel_id=1, source_target_pairs={{0,2},{1,3},{2,0},{3,1},{4,6},{5,7},{6,4},{7,5},{8,10},{9,11},{10,... | collective-permute-start | bytes 995336 | tf_op jit(solution)/shard_map/ppermute | solution.py:541
  5.0 24.6 %collective-permute-start = (bf16[144,1152]{1,0:T(8,128)(2,1)S(1)}, bf16[144,1152]{1,0:T(8,128)(2,1)S(1)}, u32[]{:S(2)}, u32[]{:S(2)}) collective-permute-start(bf16[144,1152]{1,0:T(8,128)(2,1)S(1)} %get-tuple-element.54.refs_0_), channel_id=1, source_target_pairs={{0,1},{1,0},{2,3},{3,2},{4,5},{5,4},{6,7},{7,6},{8,9},{9,8},{10,11... | collective-permute-start | bytes 995336 | tf_op jit(solution)/shard_map/ppermute | solution.py:541
  7.1 5.9 %copy-start.13 = (s32[576]{0:T(1024)S(1)}, s32[576]{0:T(1024)}, u32[]{:S(2)}) copy-start(s32[576]{0:T(1024)} %param.17) | copy-start | bytes 6916
  7.1 17.6 %all-to-all-start = ((s16[8,176,128]{2,1,0:T(8,128)(2,1)}), s16[8,176,128]{2,1,0:T(8,128)(2,1)S(1)}, u32[]{:S(2)}, u32[]{:S(2)}) async-start(s16[8,176,128]{2,1,0:T(8,128)(2,1)} %shard_map.91), calls=%async_computation | async-start | bytes 720896 | tf_op jit(solution)/shard_map/all_to_all | solution.py:559
  13.0 0.7 copy-start.14
  13.7 0.7 copy-start.15
  14.5 0.7 copy-start.2
  15.9 13.8 %collective-permute-start.2 = (bf16[144,1152]{1,0:T(8,128)(2,1)S(1)}, bf16[144,1152]{1,0:T(8,128)(2,1)S(1)}, u32[]{:S(2)}, u32[]{:S(2)}) collective-permute-start(bf16[144,1152]{1,0:T(8,128)(2,1)S(1)} %collective-permute-done.1.refs_2_), channel_id=1, source_target_pairs={{0,1},{1,0},{2,3},{3,2},{4,5},{5,4},{6,7},{7,6},{8,9},{9,8},{10,11... | collective-permute-start | bytes 995336 | tf_op jit(solution)/shard_map/ppermute | solution.py:541
  26.0 14.8 %all-to-all-start.1 = ((s16[8,176,128]{2,1,0:T(8,128)(2,1)}), s16[8,176,128]{2,1,0:T(8,128)(2,1)S(1)}, u32[]{:S(2)}, u32[]{:S(2)}) async-start(s16[8,176,128]{2,1,0:T(8,128)(2,1)} %shard_map.93), calls=%async_computation.1 | async-start | bytes 720896 | tf_op jit(solution)/shard_map/all_to_all | solution.py:559
  31.2 0.7 copy-start.4
  41.1 13.9 %collective-permute-start.4 = (bf16[144,1152]{1,0:T(8,128)(2,1)S(1)}, bf16[144,1152]{1,0:T(8,128)(2,1)S(1)}, u32[]{:S(2)}, u32[]{:S(2)}) collective-permute-start(bf16[144,1152]{1,0:T(8,128)(2,1)S(1)} %get-tuple-element.62.refs_0_), channel_id=1, source_target_pairs={{0,1},{1,0},{2,3},{3,2},{4,5},{5,4},{6,7},{7,6},{8,9},{9,8},{10,11... | collective-permute-start | bytes 995336 | tf_op jit(solution)/shard_map/ppermute | solution.py:541
  41.2 10.2 %collective-permute-start.3 = (bf16[144,1152]{1,0:T(8,128)(2,1)S(1)}, bf16[144,1152]{1,0:T(8,128)(2,1)S(1)}, u32[]{:S(2)}, u32[]{:S(2)}) collective-permute-start(bf16[144,1152]{1,0:T(8,128)(2,1)S(1)} %get-tuple-element.62.refs_0_), channel_id=1, source_target_pairs={{0,2},{1,3},{2,0},{3,1},{4,6},{5,7},{6,4},{7,5},{8,10},{9,11},{10,... | collective-permute-start | bytes 995336 | tf_op jit(solution)/shard_map/ppermute | solution.py:541
  42.4 0.7 copy-start.6
  43.0 0.7 copy-start.11
  51.4 3.6 %collective-permute-start.5 = (bf16[144,1152]{1,0:T(8,128)(2,1)S(1)}, bf16[144,1152]{1,0:T(8,128)(2,1)S(1)}, u32[]{:S(2)}, u32[]{:S(2)}) collective-permute-start(bf16[144,1152]{1,0:T(8,128)(2,1)S(1)} %collective-permute-done.3.refs_2_), channel_id=1, source_target_pairs={{0,1},{1,0},{2,3},{3,2},{4,5},{5,4},{6,7},{7,6},{8,9},{9,8},{10,11... | collective-permute-start | bytes 995336 | tf_op jit(solution)/shard_map/ppermute | solution.py:541
  51.4 12.0 %all-to-all-start.2 = ((s16[8,88,128]{2,1,0:T(8,128)(2,1)}), s16[8,88,128]{2,1,0:T(8,128)(2,1)S(1)}, u32[]{:S(2)}, u32[]{:S(2)}) async-start(s16[8,88,128]{2,1,0:T(8,128)(2,1)} %get-tuple-element.71), calls=%async_computation.2 | async-start | bytes 360448 | tf_op jit(solution)/shard_map/all_to_all | solution.py:559
  55.0 0.9 copy-start.7
  56.0 0.9 copy-start.12
  85.7 10.5 %collective-permute-start.7 = (bf16[144,576]{1,0:T(8,128)(2,1)S(1)}, bf16[144,576]{1,0:T(8,128)(2,1)S(1)}, u32[]{:S(2)}, u32[]{:S(2)}) collective-permute-start(bf16[144,576]{1,0:T(8,128)(2,1)S(1)} %get-tuple-element.77.refs_0_), channel_id=1, source_target_pairs={{0,1},{1,0},{2,3},{3,2},{4,5},{5,4},{6,7},{7,6},{8,9},{9,8},{10,11... | collective-permute-start | bytes 497672 | tf_op jit(solution)/shard_map/ppermute | solution.py:541
  85.7 7.0 %collective-permute-start.6 = (bf16[144,576]{1,0:T(8,128)(2,1)S(1)}, bf16[144,576]{1,0:T(8,128)(2,1)S(1)}, u32[]{:S(2)}, u32[]{:S(2)}) collective-permute-start(bf16[144,576]{1,0:T(8,128)(2,1)S(1)} %get-tuple-element.77.refs_0_), channel_id=1, source_target_pairs={{0,2},{1,3},{2,0},{3,1},{4,6},{5,7},{6,4},{7,5},{8,10},{9,11},{10,... | collective-permute-start | bytes 497672 | tf_op jit(solution)/shard_map/ppermute | solution.py:541
  86.6 0.7 copy-start.9
  87.3 8.9 %copy-start.8 = (bf16[144,576]{1,0:T(8,128)(2,1)S(1)}, bf16[144,576]{1,0:T(8,128)(2,1)}, u32[]{:S(2)}) copy-start(bf16[144,576]{1,0:T(8,128)(2,1)} %copy-done.6) | copy-start | bytes 497668
  92.8 3.4 %collective-permute-start.8 = (bf16[144,576]{1,0:T(8,128)(2,1)S(1)}, bf16[144,576]{1,0:T(8,128)(2,1)S(1)}, u32[]{:S(2)}, u32[]{:S(2)}) collective-permute-start(bf16[144,576]{1,0:T(8,128)(2,1)S(1)} %collective-permute-done.6.refs_2_), channel_id=1, source_target_pairs={{0,1},{1,0},{2,3},{3,2},{4,5},{5,4},{6,7},{7,6},{8,9},{9,8},{10,11... | collective-permute-start | bytes 497672 | tf_op jit(solution)/shard_map/ppermute | solution.py:541
  92.8 12.0 %all-to-all-start.5 = ((s16[8,88,128]{2,1,0:T(8,128)(2,1)}), s16[8,88,128]{2,1,0:T(8,128)(2,1)S(1)}, u32[]{:S(2)}, u32[]{:S(2)}) async-start(s16[8,88,128]{2,1,0:T(8,128)(2,1)} %get-tuple-element.82), calls=%async_computation.5 | async-start | bytes 360448 | tf_op jit(solution)/shard_map/all_to_all | solution.py:559
  96.2 0.9 copy-start.10
  97.1 7.6 %copy-start.3 = (f32[1,576]{1,0:T(1,128)S(1)}, f32[1,576]{1,0:T(1,128)}, u32[]{:S(2)}) copy-start(f32[1,576]{1,0:T(1,128)} %occ.5) | copy-start | bytes 6916
  97.1 7.6 %copy-start.5 = (f32[144,640]{1,0:T(8,128)S(1)}, f32[144,640]{1,0:T(8,128)}, u32[]{:S(2)}) copy-start(f32[144,640]{1,0:T(8,128)} %copy-done.4) | copy-start | bytes 1105924
  104.9 5.8 %collective-permute-start.10 = (bf16[144,576]{1,0:T(8,128)(2,1)S(1)}, bf16[144,576]{1,0:T(8,128)(2,1)S(1)}, u32[]{:S(2)}, u32[]{:S(2)}) collective-permute-start(bf16[144,576]{1,0:T(8,128)(2,1)S(1)} %get-tuple-element.91.refs_0_), channel_id=1, source_target_pairs={{0,2},{1,3},{2,0},{3,1},{4,6},{5,7},{6,4},{7,5},{8,10},{9,11},{10,... | collective-permute-start | bytes 497672 | tf_op jit(solution)/shard_map/ppermute | solution.py:541
  105.5 11.0 %all-to-all-start.6 = ((s16[8,88,128]{2,1,0:T(8,128)(2,1)}), s16[8,88,128]{2,1,0:T(8,128)(2,1)S(1)}, u32[]{:S(2)}, u32[]{:S(2)}) async-start(s16[8,88,128]{2,1,0:T(8,128)(2,1)} %shard_map.102), calls=%async_computation.6 | async-start | bytes 360448 | tf_op jit(solution)/shard_map/all_to_all | solution.py:559
  108.8 18.1 %copy-start.1 = (f32[1,144,576]{2,1,0:T(8,128)S(1)}, f32[1,144,576]{2,1,0:T(8,128)}, u32[]{:S(2)}) copy-start(f32[1,144,576]{2,1,0:T(8,128)} %param.10) | copy-start | bytes 995332
  108.9 1.8 %collective-permute-start.9 = (bf16[144,576]{1,0:T(8,128)(2,1)S(1)}, bf16[144,576]{1,0:T(8,128)(2,1)S(1)}, u32[]{:S(2)}, u32[]{:S(2)}) collective-permute-start(bf16[144,576]{1,0:T(8,128)(2,1)S(1)} %get-tuple-element.91.refs_0_), channel_id=1, source_target_pairs={{0,1},{1,0},{2,3},{3,2},{4,5},{5,4},{6,7},{7,6},{8,9},{9,8},{10,11... | collective-permute-start | bytes 497672 | tf_op jit(solution)/shard_map/ppermute | solution.py:541
  110.7 5.8 %collective-permute-start.11 = (bf16[144,576]{1,0:T(8,128)(2,1)S(1)}, bf16[144,576]{1,0:T(8,128)(2,1)S(1)}, u32[]{:S(2)}, u32[]{:S(2)}) collective-permute-start(bf16[144,576]{1,0:T(8,128)(2,1)S(1)} %collective-permute-done.10.refs_2_), channel_id=1, source_target_pairs={{0,1},{1,0},{2,3},{3,2},{4,5},{5,4},{6,7},{7,6},{8,9},{9,8},{10,11... | collective-permute-start | bytes 497672 | tf_op jit(solution)/shard_map/ppermute | solution.py:541
